TPU v7x, 128 devices: a whole 4x4x4 slice. The times are simulated.
128 devices in a mesh: emb: 128 (over z, y, x, core).
Axes of the slice: x: 4, y: 4, z: 4, core: 2. Of those that a mesh axis runs over, the one named last changes fastest.
Arguments:
- token_ids: int32 [16384], P('emb')
- hot_ids: int32 [2048], replicated
- x_in: bfloat16 [16384, 3072], P('emb')
- d_out: bfloat16 [16384, 3072], P('emb')
- emb_table: bfloat16 [2, 128256, 256], P(None, 'emb')
- hot_table: bfloat16 [2, 2048, 256], replicated
- w_up: bfloat16 [2, 3072, 8192], replicated
- w_down: bfloat16 [2, 8192, 3072], replicated
- w_gate: bfloat16 [2, 3072, 256], replicated
- w_proj: bfloat16 [2, 256, 3072], replicated
Outputs:
- output 1: bfloat16 [16384, 3072], P('emb')
- output 2: float32 [2, 128256, 256], P(None, 'emb')
- output 3: float32 [2, 2048, 256], replicated
All inputs are finite; a program needn't handle non-finite values.
Results may differ from a plain program's by a relative error of at most 0.0121393.
Values are sent between devices in bfloat16 or wider.
A program may use at most 1 GiB of HBM per device.

v0:
```python
import jax
import jax.numpy as jnp
from jax import lax
from jax.sharding import PartitionSpec as P

NORM_EPS = 1e-6


def gelu_back(pre_act, cot_in):
    _, pull = jax.vjp(jax.nn.gelu, pre_act.astype(jnp.float32))
    return pull(cot_in)[0]


def dense_parts(resid, w_up, w_gate):
    resid_f = resid.astype(jnp.float32)
    inv_rms = lax.rsqrt(jnp.mean(resid_f * resid_f, axis=-1, keepdims=True) + NORM_EPS)
    normed = (resid_f * inv_rms).astype(jnp.bfloat16)
    hidden = jnp.dot(normed, w_up, preferred_element_type=jnp.float32).astype(jnp.bfloat16)
    gate_pre = jnp.dot(normed, w_gate, preferred_element_type=jnp.float32).astype(jnp.bfloat16)
    return resid_f, inv_rms, hidden, gate_pre


def layer_forward(resid, emb_rows, w_up, w_down, w_gate, w_proj):
    resid_f, _, hidden, gate_pre = dense_parts(resid, w_up, w_gate)
    activated = jax.nn.gelu(hidden.astype(jnp.float32)).astype(jnp.bfloat16)
    mlp_out = jnp.dot(activated, w_down, preferred_element_type=jnp.float32).astype(jnp.bfloat16)
    gate = jax.nn.gelu(gate_pre.astype(jnp.float32)).astype(jnp.bfloat16)
    mixed = (gate.astype(jnp.float32) * emb_rows.astype(jnp.float32)).astype(jnp.bfloat16)
    projected = jnp.dot(mixed, w_proj, preferred_element_type=jnp.float32).astype(jnp.bfloat16)
    return (resid_f + mlp_out.astype(jnp.float32) + projected.astype(jnp.float32)).astype(jnp.bfloat16)


def layer_backward(resid, emb_rows, d_next, w_up, w_down, w_gate, w_proj):
    resid_f, inv_rms, hidden, gate_pre = dense_parts(resid, w_up, w_gate)
    gate = jax.nn.gelu(gate_pre.astype(jnp.float32)).astype(jnp.bfloat16)
    d_cast = d_next.astype(jnp.bfloat16)
    d_mixed = jnp.einsum('nd,ed->ne', d_cast, w_proj, preferred_element_type=jnp.float32)
    d_rows = gate.astype(jnp.float32) * d_mixed
    d_gpre = gelu_back(gate_pre, d_mixed * emb_rows.astype(jnp.float32))
    d_hidden = gelu_back(hidden, jnp.einsum('nd,fd->nf', d_cast, w_down, preferred_element_type=jnp.float32))
    d_normed = (jnp.einsum('nf,df->nd', d_hidden.astype(jnp.bfloat16), w_up, preferred_element_type=jnp.float32)
                + jnp.einsum('ne,de->nd', d_gpre.astype(jnp.bfloat16), w_gate, preferred_element_type=jnp.float32))
    inner = jnp.mean(d_normed * resid_f, axis=-1, keepdims=True)
    d_prev = d_next + inv_rms * d_normed - resid_f * (inv_rms * inv_rms * inv_rms) * inner
    return d_prev, d_rows


def solution(mesh):
    n_dev = mesh.shape['emb']

    def body(token_ids, hot_ids, x_in, d_out, emb_table, hot_table, w_up, w_down, w_gate, w_proj):
        n_loc = token_ids.shape[0]
        layers = emb_table.shape[0]
        rows_dev = emb_table.shape[1]
        emb_dim = emb_table.shape[2]
        capacity = max(8, (2 * n_loc) // n_dev)
        n_slots = n_dev * capacity
        my_index = lax.axis_index('emb')
        hot_match = token_ids[:, None] == hot_ids[None, :]
        is_hot = jnp.any(hot_match, axis=1)
        hot_pick = hot_match.astype(jnp.bfloat16)
        hot_pick_f = hot_match.astype(jnp.float32)
        owner_id = token_ids // rows_dev
        to_owner = (owner_id[:, None] == jnp.arange(n_dev, dtype=jnp.int32)[None, :]) & jnp.logical_not(is_hot)[:, None]
        owner_rank = jnp.cumsum(to_owner.astype(jnp.int32), axis=0) - 1
        place = jnp.sum(jnp.where(to_owner, owner_rank, 0), axis=1)
        slot = jnp.where(is_hot, n_slots, owner_id * capacity + place)
        send_ids = jnp.full((n_slots,), -1, jnp.int32).at[slot].set(token_ids, mode='drop')
        slot_tok = jnp.full((n_slots,), -1, jnp.int32).at[slot].set(jnp.arange(n_loc, dtype=jnp.int32), mode='drop')
        recv_ids = lax.all_to_all(send_ids.reshape(n_dev, capacity), 'emb', 0, 0, tiled=True).reshape(n_slots)
        served_ok = recv_ids >= 0
        local_row = jnp.where(served_ok, recv_ids - my_index * rows_dev, 0)
        pick_slot = jnp.minimum(slot, n_slots - 1)
        slot_used = slot_tok >= 0
        slot_src = jnp.maximum(slot_tok, 0)
        resid = x_in
        saved = []
        for layer_idx in range(layers):
            served = jnp.take(emb_table[layer_idx], local_row, axis=0)
            fetched = lax.all_to_all(served.reshape(n_dev, capacity, emb_dim), 'emb', 0, 0, tiled=True).reshape(n_slots, emb_dim)
            cold_rows = jnp.take(fetched, pick_slot, axis=0)
            hot_rows = jnp.dot(hot_pick, hot_table[layer_idx], preferred_element_type=jnp.float32).astype(jnp.bfloat16)
            emb_rows = jnp.where(is_hot[:, None], hot_rows, cold_rows)
            saved.append((resid, emb_rows))
            resid = layer_forward(resid, emb_rows, w_up[layer_idx], w_down[layer_idx], w_gate[layer_idx], w_proj[layer_idx])
        d_resid = d_out.astype(jnp.float32)
        d_tables = []
        d_hots = []
        for layer_idx in reversed(range(layers)):
            resid_l, rows_l = saved[layer_idx]
            d_resid, d_rows = layer_backward(resid_l, rows_l, d_resid, w_up[layer_idx], w_down[layer_idx], w_gate[layer_idx], w_proj[layer_idx])
            outgoing = jnp.where(slot_used[:, None], jnp.take(d_rows, slot_src, axis=0), 0.0)
            incoming = lax.all_to_all(outgoing.reshape(n_dev, capacity, emb_dim), 'emb', 0, 0, tiled=True).reshape(n_slots, emb_dim)
            d_tables.append(jax.ops.segment_sum(jnp.where(served_ok[:, None], incoming, 0.0), local_row, num_segments=rows_dev))
            hot_local = jnp.einsum('nh,ne->he', hot_pick_f, d_rows, precision=lax.Precision.HIGHEST, preferred_element_type=jnp.float32)
            d_hots.append(lax.psum(hot_local, 'emb'))
        return resid, jnp.stack(d_tables[::-1]), jnp.stack(d_hots[::-1])

    return jax.shard_map(body, mesh=mesh,
                         in_specs=(P('emb'), P(), P('emb', None), P('emb', None), P(None, 'emb', None), P(), P(), P(), P(), P()),
                         out_specs=(P('emb', None), P(None, 'emb', None), P()),
                         check_vma=False)
```

profile of v0, /device:TPU:1, one launch (start us, length us, event | category | flops | bytes accessed | tf_op | source)
XLA Modules:
  0.0 397.3 jit_solution(17513445792434020276)
XLA Ops:
  11.9 11.5 %all-to-all-start = ((s32[128,1,8]{2,1,0:T(1,128)}), s32[128,1,8]{2,1,0:T(1,128)S(1)}, u32[]{:S(2)}, u32[]{:S(2)}) async-start(s32[128,1,8]{2,1,0:T(1,128)} %bitcast.4), calls=%async_computation | async-start | bytes 131072 | tf_op jit(solution)/shard_map/all_to_all | solution.py:70
  23.4 3.4 fusion.266
  28.3 20.1 %fusion.46.clone.11 = bf16[128,8192]{1,0:T(8,128)(2,1)} fusion(bf16[2,3072,8192]{2,1,0:T(8,128)(2,1)} %param.22, bf16[128,3072]{1,0:T(8,128)(2,1)} %param.18, f32[128]{0:T(128)S(1)} %add_rsqrt_fusion.1), kind=kOutput, calls=%fused_computation.49.clone.clone.clone.clone.clone.clone.clone.clone.clone.2 | convolution fusion | flops 6455164928 | bytes 53215744 | tf_op jit(solution)/shard_map/dot_general | solution.py:18
  48.4 19.7 %fusion.83 = f32[128,3072]{1,0:T(8,128)} fusion(bf16[2,8192,3072]{2,1,0:T(8,128)(2,1)} %param.23, bf16[128,3072]{1,0:T(8,128)(2,1)S(1)} %copy-done.6, bf16[128,8192]{1,0:T(8,128)(2,1)} %fusion.46.clone.11), kind=kOutput, calls=%fused_computation.67 | convolution fusion | flops 6444023808 | bytes 54788096 | tf_op jit(solution)/shard_map/dot_general | solution.py:26
  68.9 5.0 %gather_fusion = bf16[1024,256]{1,0:T(8,128)(2,1)} fusion(bf16[1002,256]{1,0:T(8,128)(2,1)S(1)} %get-tuple-element.39, s32[1024]{0:T(1024)S(1)} %fusion.240), kind=kCustom, calls=%fused_computation.clone | custom fusion | bytes 1052672 | tf_op jit(solution)/shard_map/jit(_take)/gather | solution.py:79
  73.9 5.0 %gather_fusion.2 = bf16[1024,256]{1,0:T(8,128)(2,1)} fusion(bf16[1002,256]{1,0:T(8,128)(2,1)S(1)} %get-tuple-element.38, s32[1024]{0:T(1024)S(1)} %fusion.240), kind=kCustom, calls=%fused_computation.3.clone | custom fusion | bytes 1052672 | tf_op jit(solution)/shard_map/jit(_take)/gather | solution.py:79
  78.9 2.5 select_bitcast_fusion.1
  81.4 10.2 %all-to-all-start.1 = ((bf16[128,8,256]{2,1,0:T(8,128)(2,1)}), bf16[128,8,256]{2,1,0:T(8,128)(2,1)}, u32[]{:S(2)}, u32[]{:S(2)}) async-start(bf16[128,8,256]{2,1,0:T(8,128)(2,1)} %get-tuple-element.28), calls=%async_computation.1 | async-start | bytes 1048576 | tf_op jit(solution)/shard_map/all_to_all | solution.py:80
  93.3 11.4 %all-to-all-done.1 = bf16[128,8,256]{2,1,0:T(8,128)(2,1)} async-done(((bf16[128,8,256]{2,1,0:T(8,128)(2,1)}), bf16[128,8,256]{2,1,0:T(8,128)(2,1)}, u32[]{:S(2)}, u32[]{:S(2)}) %all-to-all-start.1) | async-done | bytes 524320 | tf_op jit(solution)/shard_map/all_to_all | solution.py:80
  104.7 4.5 %all-to-all-start.2 = ((bf16[128,8,256]{2,1,0:T(8,128)(2,1)}), bf16[128,8,256]{2,1,0:T(8,128)(2,1)S(1)}, u32[]{:S(2)}, u32[]{:S(2)}) async-start(bf16[128,8,256]{2,1,0:T(8,128)(2,1)} %get-tuple-element.29), calls=%async_computation.2 | async-start | bytes 1048576 | tf_op jit(solution)/shard_map/all_to_all | solution.py:80
  109.2 1.9 gather_fusion.1
  111.1 3.2 multiply_reduce_fusion.1
  114.3 19.5 %fusion.27 = f32[128,8192]{1,0:T(8,128)} fusion(bf16[2,3072,8192]{2,1,0:T(8,128)(2,1)} %param.22, f32[128,3072]{1,0:T(8,128)S(1)} %get-tuple-element.33, f32[128]{0:T(128)S(1)} %get-tuple-element.31), kind=kOutput, calls=%fused_computation.31 | convolution fusion | flops 6445334528 | bytes 56099328 | tf_op jit(solution)/shard_map/dot_general | solution.py:18
  133.8 1.9 fusion.139
  138.1 42.6 %fusion.4 = f32[128,3072]{1,0:T(8,128)} fusion(bf16[2,3072,8192]{2,1,0:T(8,128)(2,1)} %param.22, f32[128,8192]{1,0:T(8,128)} %fusion.27, bf16[128,3072]{1,0:T(8,128)(2,1)S(1)} %copy-done.3, bf16[2,8192,3072]{2,1,0:T(8,128)(2,1)} %param.23), kind=kOutput, calls=%fused_computation.14 | convolution fusion | flops 12905873408 | bytes 107216896 | tf_op jit(solution)/shard_map/nf,df->nd/dot_general | solution.py:41
  180.7 2.4 convert_multiply_fusion.2
  183.2 2.3 multiply_reduce_fusion
  186.5 3.5 gather_fusion.4
  189.9 4.7 %gather_fusion.5 = f32[1024,256]{1,0:T(8,128)} fusion(f32[128,256]{1,0:T(8,128)S(1)} %get-tuple-element.36, s32[1024]{0:T(1024)S(1)} %maximum_clamp_fusion), kind=kCustom, calls=%fused_computation.5.clone | custom fusion | bytes 2101248 | tf_op jit(solution)/shard_map/jit(_take)/gather | solution.py:92
  194.6 2.9 fusion.174
  197.6 9.9 %all-to-all-start.4 = ((f32[128,8,256]{2,1,0:T(8,128)}), f32[128,8,256]{2,1,0:T(8,128)S(1)}, u32[]{:S(2)}, u32[]{:S(2)}) async-start(f32[128,8,256]{2,1,0:T(8,128)} %get-tuple-element.27), calls=%async_computation.4 | async-start | bytes 2097152 | tf_op jit(solution)/shard_map/all_to_all | solution.py:93
  207.5 10.1 %all-reduce.3.cloned.1.call-start = ((), (), s32[]{:S(2)}) async-start(), calls=%async_computation.5 | async-start | bytes 8388608 | tf_op jit(solution)/shard_map/psum | solution.py:96
  217.7 2.4 convolution_bitcast_fusion
  220.1 2.4 convolution_bitcast_fusion.1
  222.6 3.0 fusion.68
  226.5 9.3 %all-to-all-start.3 = ((f32[128,8,256]{2,1,0:T(8,128)}), f32[128,8,256]{2,1,0:T(8,128)}, u32[]{:S(2)}, u32[]{:S(2)}) async-start(f32[128,8,256]{2,1,0:T(8,128)} %get-tuple-element.26), calls=%async_computation.3 | async-start | bytes 2097152 | tf_op jit(solution)/shard_map/all_to_all | solution.py:93
  235.8 21.0 %fusion.65 = bf16[128,3072]{1,0:T(8,128)(2,1)} fusion(f32[128,3072]{1,0:T(8,128)} %fusion.68, f32[128,3072]{1,0:T(8,128)S(1)} %get-tuple-element.33, bf16[2,8192,3072]{2,1,0:T(8,128)(2,1)} %param.23, f32[128,8192]{1,0:T(8,128)} %fusion.27), kind=kOutput, calls=%fused_computation.57 | convolution fusion | flops 6453854208 | bytes 58458112 | tf_op jit(solution)/shard_map/dot_general | solution.py:26
  256.7 8.2 %scatter_custom_fusion.3 = f32[1002,256]{1,0:T(8,128)S(1)} fusion(s32[1024]{0:T(1024)S(1)} %reshape.196, f32[128,8,256]{2,1,0:T(8,128)S(1)} %all-to-all-done.4, f32[]{:T(128)} %constant.18.clone.1, pred[1024]{0:T(1024)(128)(4,1)S(1)} %ge.36), kind=kCustom, calls=%fused_computation.126 | custom fusion | flops 524288 | bytes 2076672 | tf_op jit(solution)/shard_map/scatter-add | solution.py:94
  265.0 8.7 %scatter_custom_fusion.2 = f32[1002,256]{1,0:T(8,128)S(1)} fusion(s32[1024]{0:T(1024)S(1)} %reshape.196, f32[128,8,256]{2,1,0:T(8,128)} %all-to-all-done.3, f32[]{:T(128)} %constant.18.clone.1, pred[1024]{0:T(1024)(128)(4,1)S(1)} %ge.36), kind=kCustom, calls=%fused_computation.128 | custom fusion | flops 524288 | bytes 2076672 | tf_op jit(solution)/shard_map/scatter-add | solution.py:94
  273.9 2.9 copy.26
  276.8 109.0 %all-reduce.3.cloned.1.call-done = (f32[1,2048,256]{2,1,0:T(8,128)}, f32[1,2048,256]{2,1,0:T(8,128)}) async-done(((f32[1,2048,256]{2,1,0:T(8,128)}, f32[1,2048,256]{2,1,0:T(8,128)}), (f32[1,2048,256]{2,1,0:T(8,128)}, f32[1,2048,256]{2,1,0:T(8,128)})) %all-reduce.3.cloned.1.call-update) | async-done | bytes 4194320 | tf_op jit(solution)/shard_map/psum | solution.py:96
  385.8 4.5 %pad_maximum_fusion = f32[2,2048,256]{2,1,0:T(8,128)} fusion(f32[1,2048,256]{2,1,0:T(8,128)} %get-tuple-element.17, f32[1,2048,256]{2,1,0:T(8,128)} %get-tuple-element.18), kind=kLoop, calls=%fused_computation.50 | loop fusion | flops 1048576 | bytes 8388608 | tf_op jit(solution)/shard_map/stack | solution.py:97
  (55 shorter events, 13.2 us)
Async XLA Ops:
  7.2 19.6 %copy-start.5 = (bf16[128,3072]{1,0:T(8,128)(2,1)S(1)}, bf16[128,3072]{1,0:T(8,128)(2,1)}, u32[]{:S(2)}) copy-start(bf16[128,3072]{1,0:T(8,128)(2,1)} %param.18) | copy-start | bytes 2359300
  11.9 56.2 %all-to-all-start = ((s32[128,1,8]{2,1,0:T(1,128)}), s32[128,1,8]{2,1,0:T(1,128)S(1)}, u32[]{:S(2)}, u32[]{:S(2)}) async-start(s32[128,1,8]{2,1,0:T(1,128)} %bitcast.4), calls=%async_computation | async-start | bytes 131072 | tf_op jit(solution)/shard_map/all_to_all | solution.py:70
  28.3 20.1 %copy-start.6 = (bf16[128,3072]{1,0:T(8,128)(2,1)S(1)}, bf16[128,3072]{1,0:T(8,128)(2,1)}, u32[]{:S(2)}) copy-start(bf16[128,3072]{1,0:T(8,128)(2,1)} %param.18) | copy-start | bytes 2359300
  78.9 12.8 %copy-start.1 = (bf16[2,3072,256]{2,1,0:T(8,128)(2,1)S(1)}, bf16[2,3072,256]{2,1,0:T(8,128)(2,1)}, u32[]{:S(2)}) copy-start(bf16[2,3072,256]{2,1,0:T(8,128)(2,1)} %param.24) | copy-start | bytes 9437188
  81.4 29.7 %copy-start.7 = (s32[2048]{0:T(1024)S(1)}, s32[2048]{0:T(1024)}, u32[]{:S(2)}) copy-start(s32[2048]{0:T(1024)} %param.17) | copy-start | bytes 24580
  81.4 29.7 %copy-start.8 = (s32[128]{0:T(128)S(1)}, s32[128]{0:T(128)}, u32[]{:S(2)}) copy-start(s32[128]{0:T(128)} %param.16) | copy-start | bytes 1540
  81.4 23.3 %all-to-all-start.1 = ((bf16[128,8,256]{2,1,0:T(8,128)(2,1)}), bf16[128,8,256]{2,1,0:T(8,128)(2,1)}, u32[]{:S(2)}, u32[]{:S(2)}) async-start(bf16[128,8,256]{2,1,0:T(8,128)(2,1)} %get-tuple-element.28), calls=%async_computation.1 | async-start | bytes 1048576 | tf_op jit(solution)/shard_map/all_to_all | solution.py:80
  104.7 31.0 %all-to-all-start.2 = ((bf16[128,8,256]{2,1,0:T(8,128)(2,1)}), bf16[128,8,256]{2,1,0:T(8,128)(2,1)S(1)}, u32[]{:S(2)}, u32[]{:S(2)}) async-start(bf16[128,8,256]{2,1,0:T(8,128)(2,1)} %get-tuple-element.29), calls=%async_computation.2 | async-start | bytes 1048576 | tf_op jit(solution)/shard_map/all_to_all | solution.py:80
  133.8 4.4 %copy-start.3 = (bf16[128,3072]{1,0:T(8,128)(2,1)S(1)}, bf16[128,3072]{1,0:T(8,128)(2,1)}, u32[]{:S(2)}) copy-start(bf16[128,3072]{1,0:T(8,128)(2,1)} %param.19) | copy-start | bytes 2359300
  180.7 2.4 copy-start.2
  183.1 2.4 copy-start
  183.1 2.5 copy-start.4
  197.6 28.9 %all-to-all-start.4 = ((f32[128,8,256]{2,1,0:T(8,128)}), f32[128,8,256]{2,1,0:T(8,128)S(1)}, u32[]{:S(2)}, u32[]{:S(2)}) async-start(f32[128,8,256]{2,1,0:T(8,128)} %get-tuple-element.27), calls=%async_computation.4 | async-start | bytes 2097152 | tf_op jit(solution)/shard_map/all_to_all | solution.py:93
  207.5 178.3 %all-reduce.3.cloned.1.call-start = ((), (), s32[]{:S(2)}) async-start(), calls=%async_computation.5 | async-start | bytes 8388608 | tf_op jit(solution)/shard_map/psum | solution.py:96
  226.5 38.5 %all-to-all-start.3 = ((f32[128,8,256]{2,1,0:T(8,128)}), f32[128,8,256]{2,1,0:T(8,128)}, u32[]{:S(2)}, u32[]{:S(2)}) async-start(f32[128,8,256]{2,1,0:T(8,128)} %get-tuple-element.26), calls=%async_computation.3 | async-start | bytes 2097152 | tf_op jit(solution)/shard_map/all_to_all | solution.py:93
Sparse Core Ops, SparseCore 0:
  222.7 163.0 all-reduce.2
where the time goes:
time: 401 us; the launch traced here: 397 us
  matrix products  144 us (36%)
  waiting for transfers between devices  121 us (30%)
  starting transfers between devices  55.5 us (14%)
  other arithmetic  30.9 us (8%)
  local copies, waits for them, and re-layouts  30.6 us (8%)
  between operations  14.5 us (4%)
    psum x1, waiting for transfers between devices, body(): d_hots.append(lax.psum(hot_local, 'emb'))  109 us
    dot_general x1, matrix products, layer_backward(): jnp.einsum('nf,df->nd', d_hidden.astype(jnp.bfloat16), w_up, preferred_el...  42.6 us
    dot_general x2, matrix products, layer_forward(): jnp.dot(activated, w_down, preferred_element_type=jnp.float32)  40.7 us
    dot_general x2, matrix products, dense_parts(): jnp.dot(normed, w_up, preferred_element_type=jnp.float32)  39.6 us
    all_to_all x2, starting transfers between devices, body(): lax.all_to_all(outgoing.reshape(n_dev, capacity, emb_dim), 'emb', 0, 0, t...  19.2 us
    scatter-add x2, other arithmetic, body(): jax.ops.segment_sum(jnp.where(served_ok[:, None], incoming, 0.0), local_r...  17 us
    all_to_all x2, starting transfers between devices, body(): lax.all_to_all(served.reshape(n_dev, capacity, emb_dim), 'emb', 0, 0, til...  14.7 us
    all_to_all x1, starting transfers between devices, body(): lax.all_to_all(send_ids.reshape(n_dev, capacity), 'emb', 0, 0, tiled=True)  11.5 us
  transfers between devices with their start and end apart: 6, of which 3 were waited for; matrix products, arithmetic and copies ran while one was open for 31% of the time, Pallas kernels for 0%

commit v1 on v0

v1 whole, which is shorter than its diff:
```python
import functools

import jax
import jax.numpy as jnp
from jax import lax
from jax.experimental import pallas as pl
from jax.experimental.pallas import tpu as pltpu
from jax.sharding import PartitionSpec as P

NORM_EPS = 1e-6
MESH = pl.DeviceIdType.MESH
F32, BF16, I32 = jnp.float32, jnp.bfloat16, jnp.int32
ANY = pl.BlockSpec(memory_space=pl.ANY)
VM = pl.BlockSpec(memory_space=pltpu.VMEM)
GC = 0.7978845608028654
VMEM_LIMIT = 60 * 1024 * 1024


def dot_nn(a, b):
    return jnp.dot(a, b, preferred_element_type=F32)


def dot_nt(a, b):
    return lax.dot_general(a, b, (((1,), (1,)), ((), ())), preferred_element_type=F32)


def gelu(x):
    return 0.5 * x * (1.0 + jnp.tanh(GC * (x + 0.044715 * x * x * x)))


def gelu_both(x):
    x2 = x * x
    t = jnp.tanh(GC * (x + 0.044715 * x * x2))
    half = 0.5 * (1.0 + t)
    return x * half, half + 0.5 * x * (1.0 - t * t) * (GC * (1.0 + 3.0 * 0.044715 * x2))


def rms(xf):
    return lax.rsqrt(jnp.mean(xf * xf, axis=-1, keepdims=True) + NORM_EPS)


def pieces(x):
    hi = x.astype(BF16)
    rest = x - hi.astype(F32)
    mid = rest.astype(BF16)
    return hi, mid, (rest - mid.astype(F32)).astype(BF16)


def dot3(oh, x):
    hi, mid, lo = pieces(x)
    return dot_nn(oh, hi) + dot_nn(oh, mid) + dot_nn(oh, lo)


def rcopy(src, dst, ssem, rsem, dev):
    return pltpu.make_async_remote_copy(src_ref=src, dst_ref=dst, send_sem=ssem, recv_sem=rsem,
                                        device_id=(dev,), device_id_type=MESH)


def pair_barrier(partner):
    bar = pltpu.get_barrier_semaphore()
    pl.semaphore_signal(bar, inc=1, device_id=(partner,), device_id_type=MESH)
    return bar


N_UP = 8
N_DN = 6
SLOTS = 3


def k0_body(x_ref, wg_ref, wup, wdn, m_ref, g_ref, xp, up, act, wu, wd, msend, mown, mrecv,
            su, sd, xs, xr, ms, mr):
    tok, dim = x_ref.shape
    half = act.shape[1]
    fu, nd = half // N_UP, dim // N_DN
    me = lax.axis_index('emb')
    par = lax.rem(me, 2)
    partner = me + 1 - 2 * par
    base = par * half

    def up_copy(i, slot):
        return pltpu.make_async_copy(wup.at[0, :, pl.ds(pl.multiple_of(base + i * fu, fu), fu)], wu.at[slot], su.at[slot])

    def dn_copy(i, slot):
        return pltpu.make_async_copy(wdn.at[0, pl.ds(pl.multiple_of(base, half), half), pl.ds(pl.multiple_of(i * nd, nd), nd)],
                                     wd.at[slot], sd.at[slot])

    for i in range(SLOTS):
        up_copy(i, i).start()
    bar = pair_barrier(partner)
    pl.semaphore_wait(bar, 1)
    xsend = rcopy(x_ref, xp, xs, xr, partner)
    xsend.start()
    xf = x_ref[...].astype(F32)
    u = (xf * rms(xf)).astype(BF16)
    up[pl.ds(0, tok), :] = u
    g_ref[...] = gelu(dot_nn(u, wg_ref[...]).astype(BF16).astype(F32)).astype(BF16)
    xsend.wait()
    xf = xp[...].astype(F32)
    up[pl.ds(tok, tok), :] = (xf * rms(xf)).astype(BF16)

    def up_step(i, c):
        slot = lax.rem(i, SLOTS)
        up_copy(i, slot).wait()
        h = dot_nn(up[...], wu[slot]).astype(BF16).astype(F32)
        act[:, pl.ds(pl.multiple_of(i * fu, fu), fu)] = gelu(h).astype(BF16)

        @pl.when(i + SLOTS < N_UP)
        def _():
            up_copy(i + SLOTS, slot).start()

        @pl.when(i + SLOTS >= N_UP)
        def _():
            dn_copy(i + SLOTS - N_UP, i + SLOTS - N_UP).start()
        return c

    lax.fori_loop(0, N_UP, up_step, 0)

    def dn_step(i, c):
        slot = lax.rem(i, SLOTS)
        dn_copy(i, slot).wait()
        r = dot_nn(act[...], wd[slot])
        mown[i] = r[:tok]
        msend[i] = r[tok:]
        rcopy(msend.at[i], mrecv.at[i], ms.at[i], mr.at[i], partner).start()

        @pl.when(i + SLOTS < N_DN)
        def _():
            dn_copy(i + SLOTS, slot).start()
        return c

    lax.fori_loop(0, N_DN, dn_step, 0)
    for i in range(N_DN):
        rcopy(msend.at[i], mrecv.at[i], ms.at[i], mr.at[i], partner).wait()
        m_ref[:, i * nd:(i + 1) * nd] = (mown[i] + mrecv[i]).astype(BF16)


def k1_body(x_ref, m0_ref, g0_ref, e0_ref, e1_ref, d_ref, wp0_ref, wg1_ref, wp1_ref, wup, wdn,
            xo_ref, rows0_ref, rows1_ref, x1, x1p, cp, up, macc, dacc, mrecv, drecv, wu, wd,
            su, sd, xs, xr, cs, cr, ms, mr, ds, dr):
    tok, dim = x_ref.shape
    ff = wup.shape[2]
    half = ff // 2
    fu = half // N_UP
    me = lax.axis_index('emb')
    par = lax.rem(me, 2)
    partner = me + 1 - 2 * par
    base = par * half

    def up_copy(i, slot):
        return pltpu.make_async_copy(wup.at[1, :, pl.ds(pl.multiple_of(base + i * fu, fu), fu)], wu.at[slot], su.at[slot])

    def dn_copy(i, slot):
        return pltpu.make_async_copy(wdn.at[1, pl.ds(pl.multiple_of(base + i * fu, fu), fu), :], wd.at[slot], sd.at[slot])

    for i in range(SLOTS):
        up_copy(i, i).start()
        dn_copy(i, i).start()
    bar = pair_barrier(partner)
    pl.semaphore_wait(bar, 1)
    csend = rcopy(d_ref, cp.at[pl.ds(tok, tok)], cs, cr, partner)
    csend.start()
    cp[pl.ds(0, tok), :] = d_ref[...]
    q = dot_nn((g0_ref[...].astype(F32) * e0_ref[...].astype(F32)).astype(BF16), wp0_ref[...]).astype(BF16)
    x1[...] = (x_ref[...].astype(F32) + m0_ref[...].astype(F32) + q.astype(F32)).astype(BF16)
    xsend = rcopy(x1, x1p, xs, xr, partner)
    xsend.start()
    xf = x1[...].astype(F32)
    u = (xf * rms(xf)).astype(BF16)
    up[pl.ds(0, tok), :] = u
    s1 = dot_nn(u, wg1_ref[...]).astype(BF16).astype(F32)
    gs, dgs = gelu_both(s1)
    g1 = gs.astype(BF16).astype(F32)
    a1 = dot_nt(d_ref[...], wp1_ref[...])
    rows1_ref[...] = a1 * g1
    e1 = e1_ref[...].astype(F32)
    du_gate = dot_nt((dgs * (a1 * e1)).astype(BF16), wg1_ref[...])
    dacc[pl.ds(0, tok), :] = du_gate
    dacc[pl.ds(tok, tok), :] = jnp.zeros_like(du_gate)
    macc[...] = jnp.zeros_like(macc)
    xsend.wait()
    csend.wait()
    xf = x1p[...].astype(F32)
    up[pl.ds(tok, tok), :] = (xf * rms(xf)).astype(BF16)

    def step(i, c):
        slot = lax.rem(i, SLOTS)
        up_copy(i, slot).wait()
        dn_copy(i, slot).wait()
        h = dot_nn(up[...], wu[slot]).astype(BF16).astype(F32)
        a, da = gelu_both(h)
        dh = (da * dot_nt(cp[...], wd[slot])).astype(BF16)
        macc[...] += dot_nn(a.astype(BF16), wd[slot])
        dacc[...] += dot_nt(dh, wu[slot])

        @pl.when(i + SLOTS < N_UP)
        def _():
            up_copy(i + SLOTS, slot).start()
            dn_copy(i + SLOTS, slot).start()
        return c

    lax.fori_loop(0, N_UP, step, 0)
    dsend = rcopy(dacc.at[pl.ds(tok, tok)], drecv, ds, dr, partner)
    msend = rcopy(macc.at[pl.ds(tok, tok)], mrecv, ms, mr, partner)
    dsend.start()
    msend.start()
    q1 = dot_nn((g1 * e1).astype(BF16), wp1_ref[...]).astype(BF16)
    dsend.wait()
    du = dacc[pl.ds(0, tok), :] + drecv[...]
    xf = x1[...].astype(F32)
    k = rms(xf)
    inner = jnp.mean(du * xf, axis=-1, keepdims=True)
    r1 = d_ref[...].astype(F32) + k * du - xf * (k * k * k) * inner
    rows0_ref[...] = dot_nt(r1.astype(BF16), wp0_ref[...]) * g0_ref[...].astype(F32)
    msend.wait()
    m1 = (macc[pl.ds(0, tok), :] + mrecv[...]).astype(BF16)
    xo_ref[...] = (xf + m1.astype(F32) + q1.astype(F32)).astype(BF16)


def wait_bytes(ref, sem):
    pltpu.make_async_copy(ref, ref, sem).wait()


def kh_body(rows_ref, hidx_ref, slot_ref, cold_ref, dhot_ref,
            csend, crecv, rall, iall, pown, psend, precv, tsend, trecv, dh,
            asem, ar, ai, cs, cr, ds, dr, ts, tr, gs, gr, fs, fr, osem):
    n_dev = csend.shape[0]
    tok = rows_ref.shape[0]
    me = lax.axis_index('emb')
    core = lax.rem(me, 2)
    chip = me // 2
    x = lax.rem(chip, 4)
    zy = chip // 4
    z = zy // 4
    partner = me + 1 - 2 * core
    bar = pltpu.get_barrier_semaphore()

    def sig(d, c):
        pl.semaphore_signal(bar, inc=1, device_id=(lax.rem(me + d, n_dev),), device_id_type=MESH)
        return c

    lax.fori_loop(1, n_dev, sig, 0)
    rall[x] = rows_ref[...]
    iall[x] = jnp.broadcast_to(hidx_ref[...], iall.shape[1:])
    slots = lax.broadcasted_iota(I32, (n_dev * 8, tok), 0)
    oh = jnp.where(slots == slot_ref[...], 1.0, 0.0).astype(BF16)
    csend[...] = dot3(oh, rows_ref[...]).reshape(csend.shape)
    crecv[me] = csend[me]
    pl.semaphore_wait(bar, n_dev - 1)

    def a_copies(d):
        dev = (zy * 4 + lax.rem(x + d, 4)) * 2 + core
        return (rcopy(rall.at[x], rall.at[x], asem.at[0], ar, dev),
                rcopy(iall.at[x], iall.at[x], asem.at[1], ai, dev))

    for d in (1, 3, 2):
        for cpy in a_copies(d):
            cpy.start()

    def cold(d, c):
        dev = lax.rem(me + d, n_dev)
        rcopy(csend.at[dev], crecv.at[me], cs, cr, dev).start()
        return c

    lax.fori_loop(1, n_dev // 4, cold, 0)
    wait_bytes(rall.at[pl.ds(0, 3)], ar)
    wait_bytes(iall.at[pl.ds(0, 3)], ai)
    q = lax.broadcasted_iota(I32, (256, 4 * tok), 0)
    ids = jnp.concatenate([iall[i, 0:1, :] for i in range(4)], axis=1)
    rall2 = pieces(rall[...].reshape(4 * tok, rall.shape[2]))

    def partial(core_of):
        want = 16 * ((q // 16) * 8 + x * 2 + core_of) + lax.rem(q, 16)
        hot = jnp.where(want == ids, 1.0, 0.0).astype(BF16)
        return dot_nn(hot, rall2[0]) + dot_nn(hot, rall2[1]) + dot_nn(hot, rall2[2])

    psend[...] = partial(1 - core)
    dcopy = rcopy(psend, precv, ds, dr, partner)
    dcopy.start()
    pown[...] = partial(core)
    lax.fori_loop(n_dev // 4, n_dev // 2, cold, 0)
    dcopy.wait()
    tsend[...] = (pown[...] + precv[...]).reshape(tsend.shape)
    trecv[zy] = tsend[zy]

    def to_yz(d, c):
        other = lax.rem(zy + d, 16)
        rcopy(tsend.at[other], trecv.at[zy], ts, tr, (other * 4 + x) * 2 + core).start()
        return c

    lax.fori_loop(1, 16, to_yz, 0)
    lax.fori_loop(n_dev // 2, n_dev, cold, 0)
    wait_bytes(trecv.at[pl.ds(0, 15)], tr)
    yx = lax.rem(chip, 16)
    dh[z, yx, core] = jnp.sum(trecv[...], axis=0)

    def gather(d, c):
        dev = lax.rem(chip + d, n_dev // 2) * 2 + core
        rcopy(dh.at[z, yx, core], dh.at[z, yx, core], gs, gr.at[z], dev).start()
        return c

    lax.fori_loop(1, n_dev // 2, gather, 0)
    for dz in range(4):
        zz = lax.rem(z + dz, 4)
        n_blk = 15 if dz == 0 else 16
        wait_bytes(dh.at[0, pl.ds(0, n_blk), 0], gr.at[zz])
        rcopy(dh.at[zz, :, core], dh.at[zz, :, core], fs, fr, partner).start()
    ccopy = pltpu.make_async_copy(crecv, cold_ref, osem.at[2])
    wait_bytes(crecv.at[pl.ds(0, n_dev - 1)], cr)
    ccopy.start()
    wait_bytes(dh.at[:, :, 0], fr)
    outs = [pltpu.make_async_copy(dh.at[:, :, :, :, pl.ds(l * 256, 256)], dhot_ref.at[l], osem.at[l]) for l in range(2)]
    for o in outs:
        o.start()
    wait_bytes(rall.at[pl.ds(0, 3)], asem.at[0])
    wait_bytes(iall.at[pl.ds(0, 3)], asem.at[1])
    wait_bytes(csend.at[pl.ds(0, n_dev - 1)], cs)
    wait_bytes(tsend.at[pl.ds(0, 15)], ts)
    wait_bytes(csend.at[pl.ds(0, n_dev - 2)], gs)
    wait_bytes(dh.at[:, :, 0], fs)
    ccopy.wait()
    for o in outs:
        o.wait()


def kt_body(row_ref, cold_ref, out_ref):
    rows = out_ref.shape[1]
    pad = -(-rows // 16) * 16
    it = lax.broadcasted_iota(I32, (pad, row_ref.shape[1]), 0)
    oh = jnp.where(it == row_ref[...], 1.0, 0.0).astype(BF16)
    for l in range(2):
        r = dot3(oh, cold_ref[:, l * 256:(l + 1) * 256])
        out_ref[l] = r[:rows]


def params(cid):
    return pltpu.CompilerParams(collective_id=cid, has_side_effects=True, vmem_limit_bytes=VMEM_LIMIT)


def sds(shape, dt):
    return jax.ShapeDtypeStruct(shape, dt)


DMA = pltpu.SemaphoreType.DMA


def solution(mesh):
    n_dev = mesh.shape['emb']

    def body(token_ids, hot_ids, x_in, d_out, emb_table, hot_table, w_up, w_down, w_gate, w_proj):
        tok, dim = x_in.shape
        _, rows_dev, emb = emb_table.shape
        ff = w_up.shape[2]
        half = ff // 2
        fu, nd = half // N_UP, dim // N_DN
        cap = 8
        n_slots = n_dev * cap
        n_hot = hot_ids.shape[0]
        me = lax.axis_index('emb')
        hot_match = token_ids[:, None] == hot_ids[None, :]
        hidx = jnp.max(jnp.where(hot_match, jnp.arange(n_hot, dtype=I32)[None, :], -1), axis=1)
        is_hot = hidx >= 0
        owner = token_ids // rows_dev
        t = jnp.arange(tok, dtype=I32)
        earlier = (owner[:, None] == owner[None, :]) & ~is_hot[None, :] & (t[None, :] < t[:, None])
        rank = jnp.sum(earlier.astype(I32), axis=1)
        slot = jnp.where(is_hot, -1, owner * cap + rank)
        slot_match = jnp.arange(n_slots, dtype=I32)[:, None] == slot[None, :]
        send_ids = jnp.sum(jnp.where(slot_match, token_ids[None, :] + 1, 0), axis=1) - 1
        recv_ids = lax.all_to_all(send_ids.reshape(n_dev, cap), 'emb', 0, 0, tiled=True).reshape(n_slots)
        local_row = jnp.where(recv_ids >= 0, recv_ids - me * rows_dev, -1)
        row_match = (local_row[:, None] == jnp.arange(rows_dev, dtype=I32)[None, :]).astype(BF16)
        served = jnp.concatenate([dot_nn(row_match, emb_table[l]).astype(BF16) for l in range(2)], axis=1)
        fetched = lax.all_to_all(served.reshape(n_dev, cap, 2 * emb), 'emb', 0, 0, tiled=True).reshape(n_slots, 2 * emb)

        m0, g0 = pl.pallas_call(
            k0_body,
            out_shape=(sds((tok, dim), BF16), sds((tok, emb), BF16)),
            in_specs=[VM, VM, ANY, ANY], out_specs=(VM, VM),
            scratch_shapes=[pltpu.VMEM((tok, dim), BF16), pltpu.VMEM((2 * tok, dim), BF16), pltpu.VMEM((2 * tok, half), BF16),
                            pltpu.VMEM((SLOTS, dim, fu), BF16), pltpu.VMEM((SLOTS, half, nd), BF16),
                            pltpu.VMEM((N_DN, tok, nd), F32), pltpu.VMEM((N_DN, tok, nd), F32), pltpu.VMEM((N_DN, tok, nd), F32),
                            DMA((SLOTS,)), DMA((SLOTS,)), DMA, DMA, DMA((N_DN,)), DMA((N_DN,))],
            compiler_params=params(0), name='dense0',
            cost_estimate=pl.CostEstimate(flops=2 * 2 * 2 * tok * dim * half, bytes_accessed=4 * dim * half, transcendentals=0),
        )(x_in, w_gate[0], w_up, w_down)

        cold = lax.dot_general(slot_match.astype(BF16), fetched, (((0,), (0,)), ((), ())), preferred_element_type=F32)
        hot_oh = hot_match.astype(BF16)
        e = [(cold[:, l * emb:(l + 1) * emb] + dot_nn(hot_oh, hot_table[l])).astype(BF16) for l in range(2)]

        x_out, rows0, rows1 = pl.pallas_call(
            k1_body,
            out_shape=(sds((tok, dim), BF16), sds((tok, emb), F32), sds((tok, emb), F32)),
            in_specs=[VM] * 9 + [ANY] * 2, out_specs=(VM, VM, VM),
            scratch_shapes=[pltpu.VMEM((tok, dim), BF16), pltpu.VMEM((tok, dim), BF16), pltpu.VMEM((2 * tok, dim), BF16),
                            pltpu.VMEM((2 * tok, dim), BF16), pltpu.VMEM((2 * tok, dim), F32), pltpu.VMEM((2 * tok, dim), F32),
                            pltpu.VMEM((tok, dim), F32), pltpu.VMEM((tok, dim), F32),
                            pltpu.VMEM((SLOTS, dim, fu), BF16), pltpu.VMEM((SLOTS, fu, dim), BF16),
                            DMA((SLOTS,)), DMA((SLOTS,)), DMA, DMA, DMA, DMA, DMA, DMA, DMA, DMA],
            compiler_params=params(1), name='dense1',
        )(x_in, m0, g0, e[0], e[1], d_out, w_proj[0], w_gate[1], w_proj[1], w_up, w_down)

        rows = jnp.concatenate([rows0, rows1], axis=1)
        w2 = 2 * emb
        cold_rows, d_hot = pl.pallas_call(
            kh_body,
            out_shape=(sds((n_dev, cap, w2), F32), sds((2, 4, 16, 2, 16, emb), F32)),
            in_specs=[VM] * 3, out_specs=(ANY, ANY),
            scratch_shapes=[pltpu.VMEM((n_dev, cap, w2), F32), pltpu.VMEM((n_dev, cap, w2), F32),
                            pltpu.VMEM((4, tok, w2), F32), pltpu.VMEM((4, 8, tok), I32),
                            pltpu.VMEM((256, w2), F32), pltpu.VMEM((256, w2), F32), pltpu.VMEM((256, w2), F32),
                            pltpu.VMEM((16, 16, w2), F32), pltpu.VMEM((16, 16, w2), F32),
                            pltpu.VMEM((4, 16, 2, 16, w2), F32),
                            DMA((2,)), DMA, DMA, DMA, DMA, DMA, DMA, DMA, DMA, DMA, DMA((4,)), DMA, DMA, DMA((3,))],
            compiler_params=params(2), name='exchange',
        )(rows, hidx.reshape(1, tok), slot.reshape(1, tok))

        d_table = pl.pallas_call(
            kt_body, out_shape=sds((2, rows_dev, emb), F32),
            in_specs=[VM, VM], out_specs=VM,
            compiler_params=pltpu.CompilerParams(vmem_limit_bytes=VMEM_LIMIT), name='table_grad',
        )(local_row.reshape(1, n_slots), cold_rows.reshape(n_slots, w2))
        return x_out, d_table, d_hot.reshape(2, n_hot, emb)

    return jax.shard_map(body, mesh=mesh,
                         in_specs=(P('emb'), P(), P('emb', None), P('emb', None), P(None, 'emb', None), P(), P(), P(), P(), P()),
                         out_specs=(P('emb', None), P(None, 'emb', None), P()),
                         check_vma=False)
```

time: 401 us -> 212 us (0.53)
  Pallas kernels: 0 us -> 161 us
  matrix products: 144 us -> 4.65 us
  waiting for transfers between devices: 121 us -> 2.61 us
  starting transfers between devices: 55.5 us -> 18.7 us
  other arithmetic: 30.9 us -> 4.67 us
  between operations: 14.5 us -> 0.84 us
  local copies, waits for them, and re-layouts: 30.6 us -> 18.1 us
    pallas_call x0 -> x4, Pallas kernels: none -> 161 us  [the longest x1 89.9 us: body(): pl.pallas_call(kh_body, out_shape=(sds((n_dev, cap, w2), F32), sds((2, 4,...]
    dot_general x15 -> x5, matrix products: 144 us -> 4.65 us  [the longest x4 4.3 us: dot_nn(): return jnp.dot(a, b, preferred_element_type=F32)]
    psum x1 -> x0, waiting for transfers between devices: 109 us -> none  [body(): d_hots.append(lax.psum(hot_local, 'emb'))]
    all_to_all x5 -> x2, starting transfers between devices: 45.4 us -> 18.7 us  [the longest x1 11.5 us: body(): lax.all_to_all(send_ids.reshape(n_dev, cap), 'emb', 0, 0, tiled=True)]
    gather x6 -> x0, local copies, waits for them, and re-layouts: 20.8 us -> none  [the longest x2 9.96 us: body(): served = jnp.take(emb_table[layer_idx], local_row, axis=0)]
    scatter-add x2 -> x0, other arithmetic: 17 us -> none  [body(): jax.ops.segment_sum(jnp.where(served_ok[:, None], incoming, 0.0), local_r...]
    psum x1 -> x0, starting transfers between devices: 10.1 us -> none  [body(): d_hots.append(lax.psum(hot_local, 'emb'))]
    all_to_all x5 -> x2, waiting for transfers between devices: 12.4 us -> 2.61 us  [the longest x1 2.61 us: body(): lax.all_to_all(send_ids.reshape(n_dev, cap), 'emb', 0, 0, tiled=True)]
  transfers between devices with their start and end apart: 6 -> 2, of which waited for: 3 -> 1; matrix products, arithmetic and copies ran while one was open for 31% -> 4% of each run, Pallas kernels for 0% -> 11%
where the time goes in v1:
time: 212 us; the launch traced here: 211 us
  Pallas kernels  161 us (76%)
  starting transfers between devices  18.7 us (9%)
  local copies, waits for them, and re-layouts  18.1 us (9%)
  other arithmetic  4.67 us (2%)
  matrix products  4.65 us (2%)
  waiting for transfers between devices  2.61 us (1%)
    pallas_call x1, Pallas kernels, body(): pl.pallas_call(kh_body, out_shape=(sds((n_dev, cap, w2), F32), sds((2, 4,...  89.9 us
    pallas_call x1, Pallas kernels, body(): pl.pallas_call(k1_body, out_shape=(sds((tok, dim), BF16), sds((tok, emb),...  41.1 us
    pallas_call x1, Pallas kernels, body(): pl.pallas_call(k0_body, out_shape=(sds((tok, dim), BF16), sds((tok, emb),...  24.1 us
    all_to_all x1, starting transfers between devices, body(): lax.all_to_all(send_ids.reshape(n_dev, cap), 'emb', 0, 0, tiled=True)  11.5 us
    unnamed x21, local copies, waits for them, and re-layouts  7.55 us
    all_to_all x1, starting transfers between devices, body(): lax.all_to_all(served.reshape(n_dev, cap, 2 * emb), 'emb', 0, 0, tiled=True)  7.17 us
    pallas_call x1, Pallas kernels, body(): pl.pallas_call(kt_body, out_shape=sds((2, rows_dev, emb), F32), in_specs=...  6.38 us
    dot_general x4, matrix products, dot_nn(): return jnp.dot(a, b, preferred_element_type=F32)  4.3 us
  transfers between devices with their start and end apart: 2, of which 1 were waited for; matrix products, arithmetic and copies ran while one was open for 4% of the time, Pallas kernels for 11%

profile of v1, /device:TPU:1, one launch (start us, length us, event | category | flops | bytes accessed | tf_op | source)
XLA Modules:
  0.0 210.9 jit_solution(7999483240650457610)
XLA Ops:
  0.6 0.7 and_select_fusion
  1.3 1.0 fusion.22
  2.3 0.2 convert_reduce_fusion
  2.5 0.2 select_reduce_fusion
  2.7 0.7 sub.33
  3.4 11.5 %all-to-all-start = ((s32[128,1,8]{2,1,0:T(1,128)}), s32[128,1,8]{2,1,0:T(1,128)S(1)}, u32[]{:S(2)}, u32[]{:S(2)}) async-start(s32[128,1,8]{2,1,0:T(1,128)} %bitcast.1), calls=%async_computation | async-start | bytes 131072 | tf_op jit(solution)/shard_map/all_to_all | solution.py:369
  14.9 0.0 copy-start.2
  15.0 3.9 %slice_bitcast_fusion.1 = (bf16[3072,256]{1,0:T(8,128)(2,1)}, bf16[3072,256]{1,0:T(8,128)(2,1)}) fusion(bf16[2,3072,256]{2,1,0:T(8,128)(2,1)} %param.18), kind=kLoop, calls=%fused_computation.11 | loop fusion | bytes 6291456 | tf_op jit(solution)/shard_map/squeeze | solution.py:401
  18.9 1.8 slice_bitcast_fusion
  20.7 1.4 fusion.36
  22.2 2.6 %all-to-all-done = s32[128,1,8]{2,1,0:T(1,128)S(1)} async-done(((s32[128,1,8]{2,1,0:T(1,128)}), s32[128,1,8]{2,1,0:T(1,128)S(1)}, u32[]{:S(2)}, u32[]{:S(2)}) %all-to-all-start) | async-done | bytes 4128 | tf_op jit(solution)/shard_map/all_to_all | solution.py:369
  24.8 0.5 broadcast.77
  25.3 0.9 fusion.35
  26.1 0.1 select_n.43
  26.2 1.2 fusion.8
  27.4 1.2 fusion.9
  28.6 0.1 pad_maximum_fusion
  28.6 1.3 copy.26
  30.0 7.2 %all-to-all-start.1 = ((bf16[128,8,512]{2,1,0:T(8,128)(2,1)}), bf16[128,8,512]{2,1,0:T(8,128)(2,1)S(1)}, u32[]{:S(2)}, u32[]{:S(2)}) async-start(bf16[128,8,512]{2,1,0:T(8,128)(2,1)} %bitcast.4), calls=%async_computation.1 | async-start | bytes 2097152 | tf_op jit(solution)/shard_map/all_to_all | solution.py:373
  37.1 0.0 copy-start.5
  37.2 24.1 %dense0.1 = (bf16[128,3072]{1,0:T(8,128)(2,1)}, bf16[128,256]{1,0:T(8,128)(2,1)}) custom-call(bf16[128,3072]{1,0:T(8,128)(2,1)} %x_ref.3, bf16[3072,256]{1,0:T(8,128)(2,1)} %get-tuple-element.34.wg_ref, bf16[2,3072,8192]{2,1,0:T(8,128)(2,1)} %wup.3, bf16[2,8192,3072]{2,1,0:T(8,128)(2,1)} %wdn.3), custom_call_target="tpu_custom_call" | custom-call | flops 12884901888 | bytes 50331648 | tf_op jit(solution)/shard_map/dense0/pallas_call | solution.py:375
  61.3 0.7 select_n.44.row_ref
  62.0 0.3 fusion.25
  62.4 1.0 fusion.16.e1_ref
  63.4 1.0 fusion.19.e0_ref
  64.4 41.1 %dense1.1 = (bf16[128,3072]{1,0:T(8,128)(2,1)}, f32[128,256]{1,0:T(8,128)}, f32[128,256]{1,0:T(8,128)}) custom-call(bf16[128,3072]{1,0:T(8,128)(2,1)} %x_ref.3, bf16[128,3072]{1,0:T(8,128)(2,1)} %get-tuple-element.10.m0_ref, bf16[128,256]{1,0:T(8,128)(2,1)} %get-tuple-element.11.g0_ref, bf16[128,256]{1,0:T(8,128)(2,1)} %fusion.19.e0_ref, ...), custom_call_target="tpu_custom_call" | custom-call | tf_op jit(solution)/shard_map/dense1/pallas_call | solution.py:391
  105.4 1.7 pad_maximum_fusion.1.rows_ref
  107.1 89.9 %exchange.1 = (f32[128,8,512]{2,1,0:T(8,128)}, f32[2,4,16,2,16,256]{5,4,3,2,1,0:T(8,128)}) custom-call(f32[128,512]{1,0:T(8,128)} %pad_maximum_fusion.1.rows_ref, s32[1,128]{1,0:T(1,128)} %bitcast.34, s32[1,128]{1,0:T(1,128)} %bitcast.33), custom_call_target="tpu_custom_call" | custom-call | tf_op jit(solution)/shard_map/exchange/pallas_call | solution.py:405
  197.0 6.4 %table_grad.1 = f32[2,1002,256]{2,1,0:T(8,128)} custom-call(s32[1,1024]{1,0:T(1,128)} %select_n.44.row_ref, f32[1024,512]{1,0:T(8,128)} %bitcast.31), custom_call_target="tpu_custom_call" | custom-call | tf_op jit(solution)/shard_map/table_grad/pallas_call | solution.py:418
  203.4 4.6 %copy.27 = f32[2,1002,256]{2,0,1:T(2,128)} copy(f32[2,1002,256]{2,1,0:T(8,128)} %table_grad.1) | data formatting | bytes 4104192
  208.0 0.9 copy.36
  208.9 2.0 copy.37
  (20 shorter events, 0.1 us)
Async XLA Ops:
  2.3 16.6 %copy-start.6 = (s32[128]{0:T(128)}, s32[128]{0:T(128)S(1)}, u32[]{:S(2)}) copy-start(s32[128]{0:T(128)S(1)} %fusion.22) | copy-start | bytes 1540
  2.5 59.5 %copy-start.4 = (s32[128]{0:T(128)}, s32[128]{0:T(128)S(1)}, u32[]{:S(2)}) copy-start(s32[128]{0:T(128)S(1)} %compare_select_fusion.2) | copy-start | bytes 1540
  3.4 21.3 %all-to-all-start = ((s32[128,1,8]{2,1,0:T(1,128)}), s32[128,1,8]{2,1,0:T(1,128)S(1)}, u32[]{:S(2)}, u32[]{:S(2)}) async-start(s32[128,1,8]{2,1,0:T(1,128)} %bitcast.1), calls=%async_computation | async-start | bytes 131072 | tf_op jit(solution)/shard_map/all_to_all | solution.py:369
  14.9 3.9 %copy-start.2 = (bf16[2,256,3072]{2,1,0:T(8,128)(2,1)S(1)}, bf16[2,256,3072]{2,1,0:T(8,128)(2,1)}, u32[]{:S(2)}) copy-start(bf16[2,256,3072]{2,1,0:T(8,128)(2,1)} %param.19) | copy-start | bytes 9437188
  18.9 1.8 copy-start.1
  30.0 32.0 %all-to-all-start.1 = ((bf16[128,8,512]{2,1,0:T(8,128)(2,1)}), bf16[128,8,512]{2,1,0:T(8,128)(2,1)S(1)}, u32[]{:S(2)}, u32[]{:S(2)}) async-start(bf16[128,8,512]{2,1,0:T(8,128)(2,1)} %bitcast.4), calls=%async_computation.1 | async-start | bytes 2097152 | tf_op jit(solution)/shard_map/all_to_all | solution.py:373
  37.1 25.2 %copy-start.5 = (s32[2048]{0:T(1024)S(1)}, s32[2048]{0:T(1024)}, u32[]{:S(2)}) copy-start(s32[2048]{0:T(1024)} %param.11) | copy-start | bytes 24580
  37.2 25.2 %copy-start.7 = (s32[128]{0:T(128)S(1)}, s32[128]{0:T(128)}, u32[]{:S(2)}) copy-start(s32[128]{0:T(128)} %param.10) | copy-start | bytes 1540
  37.2 25.2 %copy-start.8 = (bf16[2,2048,256]{2,1,0:T(8,128)(2,1)S(1)}, bf16[2,2048,256]{2,1,0:T(8,128)(2,1)}, u32[]{:S(2)}) copy-start(bf16[2,2048,256]{2,1,0:T(8,128)(2,1)} %param.15) | copy-start | bytes 6291460
  197.0 11.0 %copy-start.3 = (bf16[128,3072]{1,0:T(8,128)(2,1)S(1)}, bf16[128,3072]{1,0:T(8,128)(2,1)}, u32[]{:S(2)}) copy-start(bf16[128,3072]{1,0:T(8,128)(2,1)} %get-tuple-element.42) | copy-start | bytes 2359300
  203.4 5.5 %copy-start = (f32[2,4,16,2,16,256]{5,4,3,2,1,0:T(8,128)S(1)}, f32[2,4,16,2,16,256]{5,4,3,2,1,0:T(8,128)}, u32[]{:S(2)}) copy-start(f32[2,4,16,2,16,256]{5,4,3,2,1,0:T(8,128)} %get-tuple-element.16) | copy-start | bytes 12582916

commit v2 on v0

v2 whole, which is shorter than its diff:
```python
import functools

import jax
import jax.numpy as jnp
from jax import lax
from jax.experimental import pallas as pl
from jax.experimental.pallas import tpu as pltpu
from jax.sharding import PartitionSpec as P

NORM_EPS = 1e-6
MESH = pl.DeviceIdType.MESH
F32, BF16, I32 = jnp.float32, jnp.bfloat16, jnp.int32
ANY = pl.BlockSpec(memory_space=pl.ANY)
VM = pl.BlockSpec(memory_space=pltpu.VMEM)
GC = 0.7978845608028654
VMEM_LIMIT = 63 * 1024 * 1024


def dot_nn(a, b):
    return jnp.dot(a, b, preferred_element_type=F32)


def dot_nt(a, b):
    return lax.dot_general(a, b, (((1,), (1,)), ((), ())), preferred_element_type=F32)


def gelu(x):
    return 0.5 * x * (1.0 + jnp.tanh(GC * (x + 0.044715 * x * x * x)))


def gelu_both(x):
    x2 = x * x
    t = jnp.tanh(GC * (x + 0.044715 * x * x2))
    half = 0.5 * (1.0 + t)
    return x * half, half + 0.5 * x * (1.0 - t * t) * (GC * (1.0 + 3.0 * 0.044715 * x2))


def rms(xf):
    return lax.rsqrt(jnp.mean(xf * xf, axis=-1, keepdims=True) + NORM_EPS)


def pieces(x):
    hi = x.astype(BF16)
    rest = x - hi.astype(F32)
    mid = rest.astype(BF16)
    return hi, mid, (rest - mid.astype(F32)).astype(BF16)


def dot3(oh, x):
    hi, mid, lo = pieces(x)
    return dot_nn(oh, hi) + dot_nn(oh, mid) + dot_nn(oh, lo)


def rcopy(src, dst, ssem, rsem, dev):
    return pltpu.make_async_remote_copy(src_ref=src, dst_ref=dst, send_sem=ssem, recv_sem=rsem,
                                        device_id=(dev,), device_id_type=MESH)


N_UP = 8
SLOTS = 3
CAP = 8
PIECE = 1024


def wait_bytes(ref, sem):
    pltpu.make_async_copy(ref, ref, sem).wait()


def dot_tn(a, b):
    return lax.dot_general(a, b, (((0,), (0,)), ((), ())), preferred_element_type=F32)


def main_body(rows_dev, x_ref, ids_ref, slot_ref, hidx_ref, emb_ref, hot_ref, wg_ref, wp_ref, d_hbm, wup, wdn,
              xo_ref, rid_ref, cold_ref, dhot_ref,
              up, cp, x1, x1p, act, macc, dacc, mrecv, drecv, wu, wd, ehot, g0s, g1s,
              idr, fsend, frecv, csend, crecv, rall, iall, psend, precv, tsend, trecv, dh,
              wsem, xs, xr, ids_s, ids_r, hs, hr, fs, fr, ash, ar, cs, cr, ps, pr, ts, tr, gs, gr, ks, kr, lsem):
    tok, dim = x_ref.shape
    n_dev = ids_ref.shape[0]
    half = wup.shape[2] // 2
    fu = half // N_UP
    emb = emb_ref.shape[2]
    hb = emb // 2
    me = lax.axis_index('emb')
    core = lax.rem(me, 2)
    chip = me // 2
    x = lax.rem(chip, 4)
    y = lax.rem(chip // 4, 4)
    zy = chip // 4
    z = zy // 4
    partner = me + 1 - 2 * core
    base = core * half
    own, oth = pl.ds(0, tok), pl.ds(tok, tok)

    def w_copies(layer, i, slot):
        off = pl.multiple_of(base + i * fu, fu)
        return (pltpu.make_async_copy(wup.at[layer, :, pl.ds(off, fu)], wu.at[slot], wsem.at[0, slot]),
                pltpu.make_async_copy(wdn.at[layer, pl.ds(off, fu), :], wd.at[slot], wsem.at[1, slot]))

    def w_start(layer, i, slot):
        for c in w_copies(layer, i, slot):
            c.start()

    def to_all(first, last, mk):
        def one(d, c):
            mk(lax.rem(me + d, n_dev)).start()
            return c
        lax.fori_loop(first, last, one, 0)

    for i in range(SLOTS):
        w_start(0, i, i)
    dcopy = pltpu.make_async_copy(d_hbm, cp.at[own], lsem.at[0])
    dcopy.start()
    bar = pltpu.get_barrier_semaphore()

    def sig(d, c):
        pl.semaphore_signal(bar, inc=1, device_id=(lax.rem(me + d, n_dev),), device_id_type=MESH)
        return c

    lax.fori_loop(1, n_dev, sig, 0)
    xf = x_ref[:].astype(F32)
    u = (xf * rms(xf)).astype(BF16)
    up[own, :] = u
    g0s[:] = gelu(dot_nn(u, wg_ref[0]).astype(BF16).astype(F32))
    idr[me] = ids_ref[me]
    iall[x] = jnp.broadcast_to(hidx_ref[:], iall.shape[1:])
    macc[:] = jnp.zeros_like(macc)
    pl.semaphore_wait(bar, n_dev - 1)

    xsend = rcopy(x_ref, x1p, xs.at[0], xr.at[0], partner)
    xsend.start()
    to_all(1, n_dev, lambda dev: rcopy(ids_ref.at[dev], idr.at[me], ids_s, ids_r, dev))
    for d in (1, 3, 2):
        rcopy(iall.at[x], iall.at[x], hs, hr, (zy * 4 + lax.rem(x + d, 4)) * 2 + core).start()
    dcopy.wait()
    csnd = rcopy(cp.at[own], cp.at[oth], xs.at[1], xr.at[1], partner)
    csnd.start()
    hid = lax.broadcasted_iota(I32, (hot_ref.shape[1], tok), 0)
    hoh = jnp.where(hid == hidx_ref[:], 1.0, 0.0).astype(BF16)
    for l in range(2):
        ehot[l] = dot_tn(hoh, hot_ref[l])
    xsend.wait()
    xf = x1p[:].astype(F32)
    up[oth, :] = (xf * rms(xf)).astype(BF16)

    def l0_step(i, c):
        slot = lax.rem(i, SLOTS)
        for cc in w_copies(0, i, slot):
            cc.wait()
        a = gelu(dot_nn(up[:], wu[slot]).astype(BF16).astype(F32)).astype(BF16)
        for n in range(0, dim, PIECE):
            macc[:, n:n + PIECE] += dot_nn(a, wd[slot, :, n:n + PIECE])
        nxt = i + SLOTS

        @pl.when(nxt < N_UP)
        def _():
            w_start(0, nxt, slot)

        @pl.when(nxt >= N_UP)
        def _():
            w_start(1, nxt - N_UP, slot)
        return c

    lax.fori_loop(0, 3, l0_step, 0)

    wait_bytes(idr.at[pl.ds(0, n_dev - 1)], ids_r)
    er = lax.broadcasted_iota(I32, (emb_ref.shape[1], tok), 0)

    def serve(g, c):
        s = jnp.sum(idr[pl.ds(g * 16, 16)], axis=0)
        lr = jnp.where(s > 0, s - 1 - me * rows_dev, -1)
        rid_ref[g] = lr
        oh = jnp.where(er == lr, 1.0, 0.0).astype(BF16)
        for l in range(2):
            sv = dot_tn(oh, emb_ref[l]).reshape(16, CAP, emb)
            fsend[l, pl.ds(g * 16, 16)] = jnp.concatenate([sv[:, :, :hb], sv[:, :, hb:]], axis=1).astype(BF16)
        return c

    lax.fori_loop(0, n_dev // 16, serve, 0)
    for l in range(2):
        frecv[l, me] = fsend[l, me]
        to_all(1, n_dev, lambda dev: rcopy(fsend.at[l, dev], frecv.at[l, me], fs.at[l], fr.at[l], dev))

    lax.fori_loop(3, N_UP, l0_step, 0)
    msend = rcopy(macc.at[oth], mrecv, xs.at[2], xr.at[2], partner)
    msend.start()
    sl = slot_ref[:]
    frow = lax.broadcasted_iota(I32, (n_dev * 16, tok), 0)
    where0 = jnp.where(sl >= 0, (sl // CAP) * 16 + lax.rem(sl, CAP), -16)

    def fetch(l):
        wait_bytes(frecv.at[l, pl.ds(0, n_dev - 1)], fr.at[l])
        f = frecv[l].reshape(n_dev * 16, hb)
        parts = [dot_tn(jnp.where(frow == where0 + h * CAP, 1.0, 0.0).astype(BF16), f) for h in range(2)]
        return (jnp.concatenate(parts, axis=1) + ehot[l]).astype(BF16).astype(F32)

    e0 = fetch(0)
    q = dot_nn((g0s[:].astype(BF16).astype(F32) * e0).astype(BF16), wp_ref[0]).astype(BF16).astype(F32)
    a1 = dot_nt(cp[own, :], wp_ref[1])
    msend.wait()
    m0 = (macc[own, :] + mrecv[:]).astype(BF16).astype(F32)
    x1[:] = (x_ref[:].astype(F32) + m0 + q).astype(BF16)
    csnd.wait()
    xsend1 = rcopy(x1, x1p, xs.at[3], xr.at[3], partner)
    xsend1.start()
    xf = x1[:].astype(F32)
    u = (xf * rms(xf)).astype(BF16)
    up[own, :] = u
    s1 = dot_nn(u, wg_ref[1]).astype(BF16).astype(F32)
    gfull, dgs = gelu_both(s1)
    g1 = gfull.astype(BF16).astype(F32)
    g1s[:] = g1

    def xpeer(d):
        return (zy * 4 + lax.rem(x + d, 4)) * 2 + core

    def cold_copy(l, dev):
        return rcopy(csend.at[dev], crecv.at[l, me], cs.at[l], cr.at[l], dev)

    def rows_out(l, rows):
        rall[l, x] = rows
        for d in (1, 3, 2):
            rcopy(rall.at[l, x], rall.at[l, x], ash.at[l], ar.at[l], xpeer(d)).start()

    def cold_out(l, rows):
        srow = lax.broadcasted_iota(I32, (n_dev * CAP, tok), 0)
        oh = jnp.where(srow == sl, 1.0, 0.0).astype(BF16)
        csend[:] = dot3(oh, rows).reshape(csend.shape)
        crecv[l, me] = csend[me]

    def hot_partial(l):
        wait_bytes(rall.at[l, pl.ds(0, 3)], ar.at[l])
        qi = lax.broadcasted_iota(I32, (256, 4 * tok), 0)
        ids = jnp.concatenate([iall[i, 0:1, :] for i in range(4)], axis=1)
        pc = pieces(rall[l].reshape(4 * tok, emb))

        def partial(core_of):
            want = 16 * ((qi // 16) * 8 + x * 2 + core_of) + lax.rem(qi, 16)
            hot = jnp.where(want == ids, 1.0, 0.0).astype(BF16)
            return dot_nn(hot, pc[0]) + dot_nn(hot, pc[1]) + dot_nn(hot, pc[2])

        psend[l] = partial(1 - core)
        rcopy(psend.at[l], precv.at[l], ps.at[l], pr.at[l], partner).start()
        tsend[l] = partial(core).reshape(tsend.shape[1:])

    def hot_sums(l):
        rcopy(psend.at[l], precv.at[l], ps.at[l], pr.at[l], partner).wait()
        tsend[l] = tsend[l] + precv[l].reshape(tsend.shape[1:])
        trecv[l, zy] = tsend[l, zy]

        def one(d, c):
            other = lax.rem(zy + d, 16)
            rcopy(tsend.at[l, other], trecv.at[l, zy], ts.at[l], tr.at[l], (other * 4 + x) * 2 + core).start()
            return c

        lax.fori_loop(1, 16, one, 0)

    s1c, s2c, s3c = 16 - 15 * core, 4 + 12 * core, 1 + 3 * core
    k1 = z + core * (x - z)
    k2 = y + core * (z - y)
    k3 = x + core * (y - x)

    def blk(a, b, e):
        return a * s1c + b * s2c + e * s3c

    def put(l, src_chip, dst_chip, ssem, rsem):
        ref = dh.at[l, src_chip, core]
        rcopy(ref, ref, ssem, rsem, dst_chip * 2 + core).start()

    def gather1(l):
        wait_bytes(trecv.at[l, pl.ds(0, 15)], tr.at[l])
        dh[l, chip, core] = jnp.sum(trecv[l], axis=0)
        for d in (1, 3, 2):
            put(l, chip, blk(lax.rem(k1 + d, 4), k2, k3), gs.at[l, 0], gr.at[l, 0])

    def gather2(l):
        wait_bytes(dh.at[l, pl.ds(0, 3), 0], gr.at[l, 0])
        for d in (1, 3, 2):
            for a in range(4):
                put(l, blk(a, k2, k3), blk(k1, lax.rem(k2 + d, 4), k3), gs.at[l, 1], gr.at[l, 1])

    def forward(l, e, first=0, last=16):
        def one(i, c):
            ref = dh.at[l, blk(lax.rem(i, 4), i // 4, e), core]
            rcopy(ref, ref, ks.at[l], kr.at[l], partner).start()
            return c
        lax.fori_loop(first, last, one, 0)

    def gather3(l):
        wait_bytes(dh.at[l, pl.ds(0, 12), 0], gr.at[l, 1])
        right, left = lax.rem(k3 + 1, 4), lax.rem(k3 + 3, 4)

        def one(i, c):
            src = blk(lax.rem(i, 4), i // 4, k3)
            put(l, src, blk(k1, k2, right), gs.at[l, 2], gr.at[l, 2])
            put(l, src, blk(k1, k2, left), gs.at[l, 2], gr.at[l, 3])
            return c

        lax.fori_loop(0, 16, one, 0)
        forward(l, k3)

    def gather4(l):
        right, left = lax.rem(k3 + 1, 4), lax.rem(k3 + 3, 4)
        wait_bytes(dh.at[l, pl.ds(0, 16), 0], gr.at[l, 2])

        def pass_right(i, c):
            put(l, blk(lax.rem(i, 4), i // 4, left), blk(k1, k2, right), gs.at[l, 3], gr.at[l, 4])
            return c

        lax.fori_loop(0, 8, pass_right, 0)
        wait_bytes(dh.at[l, pl.ds(0, 16), 0], gr.at[l, 3])

        def pass_left(i, c):
            put(l, blk(lax.rem(i, 4), i // 4, right), blk(k1, k2, left), gs.at[l, 3], gr.at[l, 4])
            return c

        lax.fori_loop(8, 16, pass_left, 0)
        forward(l, left)
        forward(l, right)

    def gather5(l):
        wait_bytes(dh.at[l, pl.ds(0, 16), 0], gr.at[l, 4])
        forward(l, lax.rem(k3 + 2, 4))

    def dhot_out(l):
        wait_bytes(dh.at[l, :, 0], kr.at[l])
        return pltpu.make_async_copy(dh.at[l], dhot_ref.at[l], lsem.at[1 + l])

    def cold_part(l, first, last):
        to_all(max(1, first * 16), last * 16, lambda dev: cold_copy(l, dev))

    rows1 = a1 * g1
    rows_out(1, rows1)
    cold_out(1, rows1)
    cold_part(1, 0, 8)
    macc[:] = jnp.zeros_like(macc)
    dacc[:] = jnp.zeros_like(dacc)
    xsend1.wait()
    xf = x1p[:].astype(F32)
    up[oth, :] = (xf * rms(xf)).astype(BF16)

    def l1_step(i, c):
        slot = lax.rem(i + N_UP, SLOTS)
        for cc in w_copies(1, i, slot):
            cc.wait()
        h = dot_nn(up[:], wu[slot]).astype(BF16).astype(F32)
        a, da = gelu_both(h)
        act[i] = a.astype(BF16)
        dhid = (da * dot_nt(cp[:], wd[slot])).astype(BF16)
        for n in range(0, dim, PIECE):
            dacc[:, n:n + PIECE] += dot_nt(dhid, wu[slot, n:n + PIECE, :])
        nxt = i + SLOTS

        @pl.when(nxt < N_UP)
        def _():
            w_start(1, nxt, slot)

        @pl.when(nxt >= N_UP)
        def _():
            w_copies(1, nxt - N_UP, slot)[1].start()
        return c

    def m_step(i, c):
        slot = lax.rem(i + 2 * N_UP, SLOTS)
        w_copies(1, i, slot)[1].wait()
        for n in range(0, dim, PIECE):
            macc[:, n:n + PIECE] += dot_nn(act[i], wd[slot, :, n:n + PIECE])

        @pl.when(i + SLOTS < N_UP)
        def _():
            w_copies(1, i + SLOTS, slot)[1].start()
        return c

    def m_part(first):
        lax.fori_loop(first, first + 2, m_step, 0)

    lax.fori_loop(0, 6, l1_step, 0)
    wait_bytes(iall.at[pl.ds(0, 3)], hr)
    hot_partial(1)
    e1 = fetch(1)
    du_gate = dot_nt((dgs * (a1 * e1)).astype(BF16), wg_ref[1])
    dacc[own, :] = dacc[own, :] + du_gate
    q1 = dot_nn((g1s[:] * e1).astype(BF16), wp_ref[1]).astype(BF16)
    lax.fori_loop(6, N_UP, l1_step, 0)

    dsend = rcopy(dacc.at[oth], drecv, xs.at[4], xr.at[4], partner)
    dsend.start()
    hot_sums(1)
    xf = x1[:].astype(F32)
    k = rms(xf)
    dsend.wait()
    du = dacc[own, :] + drecv[:]
    inner = jnp.mean(du * xf, axis=-1, keepdims=True)
    r1 = cp[own, :].astype(F32) + k * du - xf * (k * k * k) * inner
    rows0 = dot_nt(r1.astype(BF16), wp_ref[0]) * g0s[:].astype(BF16).astype(F32)
    rows_out(0, rows0)
    wait_bytes(csend.at[pl.ds(0, n_dev - 1)], cs.at[1])
    cold_out(0, rows0)
    cold_part(0, 0, 2)
    gather1(1)
    m_part(0)
    hot_partial(0)
    gather2(1)
    m_part(2)
    hot_sums(0)
    cold_part(0, 2, 4)
    gather3(1)
    wait_bytes(crecv.at[1, pl.ds(0, n_dev - 1)], cr.at[1])
    ccopy1 = pltpu.make_async_copy(crecv.at[1], cold_ref.at[1], lsem.at[3])
    ccopy1.start()
    m_part(4)
    gather1(0)
    cold_part(0, 4, 5)
    gather4(1)
    m_part(6)
    msend = rcopy(macc.at[oth], mrecv, xs.at[5], xr.at[5], partner)
    msend.start()
    gather2(0)
    cold_part(0, 5, 7)
    gather5(1)
    gather3(0)
    cold_part(0, 7, 8)
    out1 = dhot_out(1)
    out1.start()
    msend.wait()
    m1 = (macc[own, :] + mrecv[:]).astype(BF16)
    xo_ref[:] = (xf + m1.astype(F32) + q1.astype(F32)).astype(BF16)
    gather4(0)
    gather5(0)
    wait_bytes(crecv.at[0, pl.ds(0, n_dev - 1)], cr.at[0])
    ccopy0 = pltpu.make_async_copy(crecv.at[0], cold_ref.at[0], lsem.at[4])
    ccopy0.start()
    out0 = dhot_out(0)
    out0.start()
    wait_bytes(idr.at[pl.ds(0, n_dev - 1)], ids_s)
    wait_bytes(iall.at[pl.ds(0, 3)], hs)
    wait_bytes(csend.at[pl.ds(0, n_dev - 1)], cs.at[0])
    for l in range(2):
        wait_bytes(fsend.at[l, pl.ds(0, n_dev - 1)], fs.at[l])
        wait_bytes(rall.at[l, pl.ds(0, 3)], ash.at[l])
        wait_bytes(tsend.at[l, pl.ds(0, 15)], ts.at[l])
        for ph, n_blk in enumerate((3, 12, 32, 16)):
            wait_bytes(dh.at[l, pl.ds(0, n_blk), 0], gs.at[l, ph])
        wait_bytes(dh.at[l, :, 0], ks.at[l])
    for c in (ccopy1, ccopy0, out1, out0):
        c.wait()


def finish_body(rid_ref, cold_ref, x_hbm, dhot_hbm, dt_ref, xo_hbm, dho_hbm, xb, hb, sem):
    rows = dt_ref.shape[0] // 4
    ins = [pltpu.make_async_copy(dhot_hbm.at[l], hb.at[l], sem.at[l]) for l in range(2)]
    ins.append(pltpu.make_async_copy(x_hbm, xb, sem.at[2]))
    for c in ins:
        c.start()
    ids = jnp.concatenate([rid_ref[g] for g in range(rid_ref.shape[0])], axis=1)
    outs = [pltpu.make_async_copy(hb.at[l], dho_hbm.at[l], sem.at[3 + l]) for l in range(2)]
    outs.append(pltpu.make_async_copy(xb, xo_hbm, sem.at[5]))
    step = 336
    for l in range(2):
        pc = pieces(cold_ref[l])
        for r0 in range(0, rows, step):
            it = lax.broadcasted_iota(I32, (step, ids.shape[1]), 0) + r0
            oh = jnp.where(it == ids, 1.0, 0.0).astype(BF16)
            r = dot_nn(oh, pc[0]) + dot_nn(oh, pc[1]) + dot_nn(oh, pc[2])
            n = min(step, rows - r0)
            for t in range(2):
                dt_ref[pl.ds(r0 * 4 + t * 2 + l, n, stride=4), :] = r[:n, t * 128:(t + 1) * 128]
        if l == 0:
            for i, o in zip(ins, outs):
                i.wait()
                o.start()
    for o in outs:
        o.wait()


def sds(shape, dt):
    return jax.ShapeDtypeStruct(shape, dt)


DMA = pltpu.SemaphoreType.DMA


def solution(mesh):
    n_dev = mesh.shape['emb']

    def body(token_ids, hot_ids, x_in, d_out, emb_table, hot_table, w_up, w_down, w_gate, w_proj):
        tok, dim = x_in.shape
        _, rows_dev, emb = emb_table.shape
        half = w_up.shape[2] // 2
        fu = half // N_UP
        n_hot = hot_ids.shape[0]
        n_slots = n_dev * CAP
        me = lax.axis_index('emb')
        hot_match = token_ids[:, None] == hot_ids[None, :]
        hidx = jnp.max(jnp.where(hot_match, jnp.arange(n_hot, dtype=I32)[None, :], -1), axis=1)
        is_hot = hidx >= 0
        owner = token_ids // rows_dev
        t = jnp.arange(tok, dtype=I32)
        earlier = (owner[:, None] == owner[None, :]) & ~is_hot[None, :] & (t[None, :] < t[:, None])
        rank = jnp.sum(earlier.astype(I32), axis=1)
        slot = jnp.where(is_hot, -1, owner * CAP + rank)
        lane = lax.rem(me, 16) * CAP + rank
        o_hit = (jnp.arange(n_dev, dtype=I32)[:, None] == jnp.where(is_hot, -1, owner)[None, :]).astype(BF16)
        l_hit = t[None, :] == lane[:, None]
        want_id = token_ids + 1
        hi, lo = want_id // 512, want_id % 512
        put = [jnp.where(l_hit, v[:, None], 0).astype(BF16) for v in (hi, lo // 2, lo % 2)]
        got = [dot_nn(o_hit, v).astype(I32) for v in put]
        send_ids = got[0] * 512 + got[1] * 2 + got[2]
        emb_pad = jnp.pad(emb_table, ((0, 0), (0, -rows_dev % 16), (0, 0)))

        VMEM = pltpu.VMEM
        x_raw, rid, cold, dhot = pl.pallas_call(
            functools.partial(main_body, rows_dev),
            out_shape=(sds((tok, dim), BF16), sds((n_dev // 16, 1, 128), I32), sds((2, n_dev, CAP, emb), F32),
                       sds((2, n_dev // 2, 2, 16, emb), F32)),
            in_specs=[VM] * 8 + [ANY] * 3, out_specs=(VM, VM, ANY, ANY),
            scratch_shapes=[VMEM((2 * tok, dim), BF16), VMEM((2 * tok, dim), BF16), VMEM((tok, dim), BF16), VMEM((tok, dim), BF16), VMEM((N_UP, 2 * tok, fu), BF16),
                            VMEM((2 * tok, dim), F32), VMEM((2 * tok, dim), F32), VMEM((tok, dim), F32), VMEM((tok, dim), F32),
                            VMEM((SLOTS, dim, fu), BF16), VMEM((SLOTS, fu, dim), BF16),
                            VMEM((2, tok, emb), F32), VMEM((tok, emb), F32), VMEM((tok, emb), F32),
                            VMEM((n_dev, 1, 128), I32), VMEM((2, n_dev, 16, 128), BF16), VMEM((2, n_dev, 16, 128), BF16),
                            VMEM((n_dev, CAP, emb), F32), VMEM((2, n_dev, CAP, emb), F32),
                            VMEM((2, 4, tok, emb), F32), VMEM((4, 8, tok), I32),
                            VMEM((2, 256, emb), F32), VMEM((2, 256, emb), F32),
                            VMEM((2, 16, 16, emb), F32), VMEM((2, 16, 16, emb), F32),
                            VMEM((2, n_dev // 2, 2, 16, emb), F32),
                            DMA((2, SLOTS)), DMA((6,)), DMA((6,)), DMA, DMA, DMA, DMA] + [DMA((2,))] * 10
            + [DMA((2, 4)), DMA((2, 5)), DMA((2,)), DMA((2,)), DMA((5,))],
            compiler_params=pltpu.CompilerParams(collective_id=0, has_side_effects=True, vmem_limit_bytes=VMEM_LIMIT),
            name='stack',
        )(x_in, send_ids.reshape(n_dev, 1, 128), slot.reshape(1, tok), hidx.reshape(1, tok), emb_pad, hot_table, w_gate, w_proj,
          d_out, w_up, w_down)

        d_table, x_out, d_hot = pl.pallas_call(
            finish_body,
            out_shape=(sds((rows_dev * 4, 128), F32), sds((tok, dim), BF16), sds((2, n_hot, emb), F32)),
            in_specs=[VM, VM, ANY, ANY], out_specs=(VM, ANY, ANY),
            scratch_shapes=[VMEM((tok, dim), BF16), VMEM((2, n_hot, emb), F32), DMA((6,))],
            compiler_params=pltpu.CompilerParams(vmem_limit_bytes=VMEM_LIMIT), name='finish',
        )(rid, cold.reshape(2, n_slots, emb), x_raw, dhot.reshape(2, n_hot, emb))
        d_table = d_table.reshape(rows_dev, 2, 2, 128).transpose(2, 0, 1, 3).reshape(2, rows_dev, emb)
        return x_out, d_table, d_hot

    return jax.shard_map(body, mesh=mesh,
                         in_specs=(P('emb'), P(), P('emb', None), P('emb', None), P(None, 'emb', None), P(), P(), P(), P(), P()),
                         out_specs=(P('emb', None), P(None, 'emb', None), P()),
                         check_vma=False)
```

time: 401 us -> 138 us (0.34)
  matrix products: 144 us -> 1.3 us
  Pallas kernels: 0 us -> 130 us
  waiting for transfers between devices: 121 us -> 0 us
  starting transfers between devices: 55.5 us -> 0 us
  local copies, waits for them, and re-layouts: 30.6 us -> 2.39 us
  other arithmetic: 30.9 us -> 3.03 us
  between operations: 14.5 us -> 0.85 us
    dot_general x15 -> x3, matrix products: 144 us -> 1.3 us  [dot_nn(): return jnp.dot(a, b, preferred_element_type=F32)]
    pallas_call x0 -> x2, Pallas kernels: none -> 130 us  [the longest x1 122 us: body(): pl.pallas_call(functools.partial(main_body, rows_dev), out_shape=(sds((to...]
    psum x1 -> x0, waiting for transfers between devices: 109 us -> none  [body(): d_hots.append(lax.psum(hot_local, 'emb'))]
    all_to_all x5 -> x0, starting transfers between devices: 45.4 us -> none  [the longest x2 19.2 us: body(): lax.all_to_all(outgoing.reshape(n_dev, capacity, emb_dim), 'emb', 0, 0, t...]
    gather x6 -> x0, local copies, waits for them, and re-layouts: 20.8 us -> none  [the longest x2 9.96 us: body(): served = jnp.take(emb_table[layer_idx], local_row, axis=0)]
    scatter-add x2 -> x0, other arithmetic: 17 us -> none  [body(): jax.ops.segment_sum(jnp.where(served_ok[:, None], incoming, 0.0), local_r...]
    all_to_all x5 -> x0, waiting for transfers between devices: 12.4 us -> none  [the longest x2 11.4 us: body(): lax.all_to_all(served.reshape(n_dev, capacity, emb_dim), 'emb', 0, 0, til...]
    psum x1 -> x0, starting transfers between devices: 10.1 us -> none  [body(): d_hots.append(lax.psum(hot_local, 'emb'))]
  transfers between devices with their start and end apart: 6 -> 0, of which waited for: 3 -> 0; matrix products, arithmetic and copies ran while one was open for 31% -> 0% of each run, Pallas kernels for 0% -> 0%
where the time goes in v2:
time: 138 us; the launch traced here: 137 us
  Pallas kernels  130 us (94%)
  other arithmetic  3.03 us (2%)
  local copies, waits for them, and re-layouts  2.39 us (2%)
    pallas_call x1, Pallas kernels, body(): pl.pallas_call(functools.partial(main_body, rows_dev), out_shape=(sds((to...  122 us
    pallas_call x1, Pallas kernels, body(): pl.pallas_call(finish_body, out_shape=(sds((rows_dev * 4, 128), F32), sds...  7.64 us

profile of v2, /device:TPU:1, one launch (start us, length us, event | category | flops | bytes accessed | tf_op | source)
XLA Modules:
  0.0 137.4 jit_solution(7361012790587035120)
XLA Ops:
  0.6 1.0 select_reduce_fusion
  1.6 0.0 copy-start
  1.6 0.7 and_select_fusion
  2.3 0.7 and_select_fusion.1
  3.0 0.2 convert_reduce_fusion
  3.2 0.5 select_bitcast_fusion
  3.7 0.2 fusion.3
  3.9 0.2 fusion.2
  4.2 0.9 fusion
  5.0 1.4 copy.15
  6.4 1.0 pad.4.emb_ref
  7.4 0.0 copy-done
  7.4 122.1 %stack.1 = (bf16[128,3072]{1,0:T(8,128)(2,1)}, s32[8,1,128]{2,1,0:T(1,128)}, f32[2,128,8,256]{3,2,1,0:T(8,128)}, f32[2,64,2,16,256]{4,3,2,1,0:T(8,128)}) custom-call(bf16[128,3072]{1,0:T(8,128)(2,1)} %x_ref.1, s32[128,1,128]{2,1,0:T(1,128)} %bitcast.13, s32[1,128]{1,0:T(1,128)} %get-tuple-element.22.slot_ref, s32[1,128]{1,0:T(1,128)} %bitcast.14, ...), custom_call_target="tpu_custom_call" | custom-call | tf_op jit(solution)/shard_map/stack/pallas_call | solution.py:513
  129.6 7.6 %finish.1 = (f32[4008,128]{1,0:T(8,128)}, bf16[128,3072]{1,0:T(8,128)(2,1)}, f32[2,2048,256]{2,1,0:T(8,128)}) custom-call(s32[8,1,128]{2,1,0:T(1,128)} %get-tuple-element.10.rid_ref, f32[2,1024,256]{2,1,0:T(8,128)} %bitcast.12, bf16[128,3072]{1,0:T(8,128)(2,1)} %get-tuple-element.12.x_hbm, f32[2,2048,256]{2,1,0:T(8,128)} %bitcast.11), custom_call_target="tpu_custom_call" | custom-call | tf_op jit(solution)/shard_map/finish/pallas_call | solution.py:535
  (1 shorter events, 0.0 us)
Async XLA Ops:
  1.6 5.8 %copy-start = (s32[128]{0:T(128)}, s32[128]{0:T(128)S(1)}, u32[]{:S(2)}) copy-start(s32[128]{0:T(128)S(1)} %select_reduce_fusion) | copy-start | bytes 1540

commit v3 on v2

--- a/solution.py
+++ b/solution.py
@@ -13,7 +13,7 @@
 ANY = pl.BlockSpec(memory_space=pl.ANY)
 VM = pl.BlockSpec(memory_space=pltpu.VMEM)
 GC = 0.7978845608028654
-VMEM_LIMIT = 63 * 1024 * 1024
+VMEM_LIMIT = 67043328
 
 
 def dot_nn(a, b):
@@ -39,6 +39,14 @@
     return lax.rsqrt(jnp.mean(xf * xf, axis=-1, keepdims=True) + NORM_EPS)
 
 
+def head(n):
+    return pl.ds(0, n)
+
+
+def one_hot(mask):
+    return jnp.where(mask, 1.0, 0.0).astype(BF16)
+
+
 def pieces(x):
     hi = x.astype(BF16)
     rest = x - hi.astype(F32)
@@ -71,10 +79,10 @@
 
 
 def main_body(rows_dev, x_ref, ids_ref, slot_ref, hidx_ref, emb_ref, hot_ref, wg_ref, wp_ref, d_hbm, wup, wdn,
-              xo_ref, rid_ref, cold_ref, dhot_ref,
+              xo_ref, dt_ref, dhot_ref,
               up, cp, x1, x1p, act, macc, dacc, mrecv, drecv, wu, wd, ehot, g0s, g1s,
-              idr, fsend, frecv, csend, crecv, rall, iall, psend, precv, tsend, trecv, dh,
-              wsem, xs, xr, ids_s, ids_r, hs, hr, fs, fr, ash, ar, cs, cr, ps, pr, ts, tr, gs, gr, ks, kr, lsem):
+              rid, idr, fsend, frecv, csend, crecv, rall, iall, psend, precv, tsend, trecv, dh,
+              wsem, xs, xr, ids_s, ids_r, hs, hr, fs, fr, ash, arl, ar, cs, cr, ps, pr, ts, tr, gs, gr, ks, kr, lsem):
     tok, dim = x_ref.shape
     n_dev = ids_ref.shape[0]
     half = wup.shape[2] // 2
@@ -90,7 +98,7 @@
     z = zy // 4
     partner = me + 1 - 2 * core
     base = core * half
-    own, oth = pl.ds(0, tok), pl.ds(tok, tok)
+    own, oth = head(tok), pl.ds(tok, tok)
 
     def w_copies(layer, i, slot):
         off = pl.multiple_of(base + i * fu, fu)
@@ -136,7 +144,7 @@
     csnd = rcopy(cp.at[own], cp.at[oth], xs.at[1], xr.at[1], partner)
     csnd.start()
     hid = lax.broadcasted_iota(I32, (hot_ref.shape[1], tok), 0)
-    hoh = jnp.where(hid == hidx_ref[:], 1.0, 0.0).astype(BF16)
+    hoh = one_hot(hid == hidx_ref[:])
     for l in range(2):
         ehot[l] = dot_tn(hoh, hot_ref[l])
     xsend.wait()
@@ -163,14 +171,14 @@
 
     lax.fori_loop(0, 3, l0_step, 0)
 
-    wait_bytes(idr.at[pl.ds(0, n_dev - 1)], ids_r)
+    wait_bytes(idr.at[head(n_dev - 1)], ids_r)
     er = lax.broadcasted_iota(I32, (emb_ref.shape[1], tok), 0)
 
     def serve(g, c):
         s = jnp.sum(idr[pl.ds(g * 16, 16)], axis=0)
         lr = jnp.where(s > 0, s - 1 - me * rows_dev, -1)
-        rid_ref[g] = lr
-        oh = jnp.where(er == lr, 1.0, 0.0).astype(BF16)
+        rid[g] = lr
+        oh = one_hot(er == lr)
         for l in range(2):
             sv = dot_tn(oh, emb_ref[l]).reshape(16, CAP, emb)
             fsend[l, pl.ds(g * 16, 16)] = jnp.concatenate([sv[:, :, :hb], sv[:, :, hb:]], axis=1).astype(BF16)
@@ -189,9 +197,9 @@
     where0 = jnp.where(sl >= 0, (sl // CAP) * 16 + lax.rem(sl, CAP), -16)
 
     def fetch(l):
-        wait_bytes(frecv.at[l, pl.ds(0, n_dev - 1)], fr.at[l])
+        wait_bytes(frecv.at[l, head(n_dev - 1)], fr.at[l])
         f = frecv[l].reshape(n_dev * 16, hb)
-        parts = [dot_tn(jnp.where(frow == where0 + h * CAP, 1.0, 0.0).astype(BF16), f) for h in range(2)]
+        parts = [dot_tn(one_hot(frow == where0 + h * CAP), f) for h in range(2)]
         return (jnp.concatenate(parts, axis=1) + ehot[l]).astype(BF16).astype(F32)
 
     e0 = fetch(0)
@@ -219,24 +227,33 @@
 
     def rows_out(l, rows):
         rall[l, x] = rows
-        for d in (1, 3, 2):
-            rcopy(rall.at[l, x], rall.at[l, x], ash.at[l], ar.at[l], xpeer(d)).start()
+        rcopy(rall.at[l, x], rall.at[l, x], ash.at[l], ar.at[l, 0], xpeer(1)).start()
+        rcopy(rall.at[l, x], rall.at[l, x], ash.at[l], ar.at[l, 1], xpeer(3)).start()
+
+    def rows_relay(l):
+        mid = tok // 2
+        wait_bytes(rall.at[l, 0], ar.at[l, 0])
+        ref = rall.at[l, lax.rem(x + 3, 4), head(mid)]
+        rcopy(ref, ref, arl.at[l], ar.at[l, 2], xpeer(1)).start()
+        wait_bytes(rall.at[l, 0], ar.at[l, 1])
+        ref = rall.at[l, lax.rem(x + 1, 4), pl.ds(mid, mid)]
+        rcopy(ref, ref, arl.at[l], ar.at[l, 2], xpeer(3)).start()
 
     def cold_out(l, rows):
         srow = lax.broadcasted_iota(I32, (n_dev * CAP, tok), 0)
-        oh = jnp.where(srow == sl, 1.0, 0.0).astype(BF16)
+        oh = one_hot(srow == sl)
         csend[:] = dot3(oh, rows).reshape(csend.shape)
         crecv[l, me] = csend[me]
 
     def hot_partial(l):
-        wait_bytes(rall.at[l, pl.ds(0, 3)], ar.at[l])
+        wait_bytes(rall.at[l, 0], ar.at[l, 2])
         qi = lax.broadcasted_iota(I32, (256, 4 * tok), 0)
         ids = jnp.concatenate([iall[i, 0:1, :] for i in range(4)], axis=1)
         pc = pieces(rall[l].reshape(4 * tok, emb))
 
         def partial(core_of):
             want = 16 * ((qi // 16) * 8 + x * 2 + core_of) + lax.rem(qi, 16)
-            hot = jnp.where(want == ids, 1.0, 0.0).astype(BF16)
+            hot = one_hot(want == ids)
             return dot_nn(hot, pc[0]) + dot_nn(hot, pc[1]) + dot_nn(hot, pc[2])
 
         psend[l] = partial(1 - core)
@@ -268,13 +285,13 @@
         rcopy(ref, ref, ssem, rsem, dst_chip * 2 + core).start()
 
     def gather1(l):
-        wait_bytes(trecv.at[l, pl.ds(0, 15)], tr.at[l])
+        wait_bytes(trecv.at[l, head(15)], tr.at[l])
         dh[l, chip, core] = jnp.sum(trecv[l], axis=0)
         for d in (1, 3, 2):
             put(l, chip, blk(lax.rem(k1 + d, 4), k2, k3), gs.at[l, 0], gr.at[l, 0])
 
     def gather2(l):
-        wait_bytes(dh.at[l, pl.ds(0, 3), 0], gr.at[l, 0])
+        wait_bytes(dh.at[l, head(3), 0], gr.at[l, 0])
         for d in (1, 3, 2):
             for a in range(4):
                 put(l, blk(a, k2, k3), blk(k1, lax.rem(k2 + d, 4), k3), gs.at[l, 1], gr.at[l, 1])
@@ -287,7 +304,7 @@
         lax.fori_loop(first, last, one, 0)
 
     def gather3(l):
-        wait_bytes(dh.at[l, pl.ds(0, 12), 0], gr.at[l, 1])
+        wait_bytes(dh.at[l, head(12), 0], gr.at[l, 1])
         right, left = lax.rem(k3 + 1, 4), lax.rem(k3 + 3, 4)
 
         def one(i, c):
@@ -301,14 +318,14 @@
 
     def gather4(l):
         right, left = lax.rem(k3 + 1, 4), lax.rem(k3 + 3, 4)
-        wait_bytes(dh.at[l, pl.ds(0, 16), 0], gr.at[l, 2])
+        wait_bytes(dh.at[l, head(16), 0], gr.at[l, 2])
 
         def pass_right(i, c):
             put(l, blk(lax.rem(i, 4), i // 4, left), blk(k1, k2, right), gs.at[l, 3], gr.at[l, 4])
             return c
 
         lax.fori_loop(0, 8, pass_right, 0)
-        wait_bytes(dh.at[l, pl.ds(0, 16), 0], gr.at[l, 3])
+        wait_bytes(dh.at[l, head(16), 0], gr.at[l, 3])
 
         def pass_left(i, c):
             put(l, blk(lax.rem(i, 4), i // 4, right), blk(k1, k2, left), gs.at[l, 3], gr.at[l, 4])
@@ -319,12 +336,25 @@
         forward(l, right)
 
     def gather5(l):
-        wait_bytes(dh.at[l, pl.ds(0, 16), 0], gr.at[l, 4])
+        wait_bytes(dh.at[l, head(16), 0], gr.at[l, 4])
         forward(l, lax.rem(k3 + 2, 4))
 
     def dhot_out(l):
         wait_bytes(dh.at[l, :, 0], kr.at[l])
         return pltpu.make_async_copy(dh.at[l], dhot_ref.at[l], lsem.at[1 + l])
+
+    def table(l):
+        wait_bytes(crecv.at[l, head(n_dev - 1)], cr.at[l])
+        ids = jnp.concatenate([rid[g] for g in range(n_dev // 16)], axis=1)
+        pc = pieces(crecv[l].reshape(n_dev * CAP, emb))
+        wide = 4 * emb
+        for j in range(4):
+            ri = lax.broadcasted_iota(I32, (2 * tok, n_dev * CAP), 0) + j * 2 * tok
+            oh = one_hot(ri == ids)
+            c0 = l * wide + j * emb
+            dacc[:, c0:c0 + emb] = dot_nn(oh, pc[0]) + dot_nn(oh, pc[1]) + dot_nn(oh, pc[2])
+        cols = pl.ds(l * wide, wide)
+        return pltpu.make_async_copy(dacc.at[:, cols], dt_ref.at[:, cols], lsem.at[3 + l])
 
     def cold_part(l, first, last):
         to_all(max(1, first * 16), last * 16, lambda dev: cold_copy(l, dev))
@@ -374,8 +404,10 @@
     def m_part(first):
         lax.fori_loop(first, first + 2, m_step, 0)
 
-    lax.fori_loop(0, 6, l1_step, 0)
-    wait_bytes(iall.at[pl.ds(0, 3)], hr)
+    lax.fori_loop(0, 3, l1_step, 0)
+    rows_relay(1)
+    lax.fori_loop(3, 6, l1_step, 0)
+    wait_bytes(iall.at[head(3)], hr)
     hot_partial(1)
     e1 = fetch(1)
     du_gate = dot_nt((dgs * (a1 * e1)).astype(BF16), wg_ref[1])
@@ -394,77 +426,71 @@
     r1 = cp[own, :].astype(F32) + k * du - xf * (k * k * k) * inner
     rows0 = dot_nt(r1.astype(BF16), wp_ref[0]) * g0s[:].astype(BF16).astype(F32)
     rows_out(0, rows0)
-    wait_bytes(csend.at[pl.ds(0, n_dev - 1)], cs.at[1])
+    wait_bytes(csend.at[head(n_dev - 1)], cs.at[1])
     cold_out(0, rows0)
     cold_part(0, 0, 2)
     gather1(1)
     m_part(0)
-    hot_partial(0)
+    rows_relay(0)
     gather2(1)
     m_part(2)
+    hot_partial(0)
+    m_part(4)
     hot_sums(0)
-    cold_part(0, 2, 4)
+    cold_part(0, 2, 5)
     gather3(1)
-    wait_bytes(crecv.at[1, pl.ds(0, n_dev - 1)], cr.at[1])
-    ccopy1 = pltpu.make_async_copy(crecv.at[1], cold_ref.at[1], lsem.at[3])
-    ccopy1.start()
-    m_part(4)
-    gather1(0)
-    cold_part(0, 4, 5)
-    gather4(1)
     m_part(6)
     msend = rcopy(macc.at[oth], mrecv, xs.at[5], xr.at[5], partner)
     msend.start()
+    gather1(0)
+    cold_part(0, 5, 7)
+    gather4(1)
     gather2(0)
-    cold_part(0, 5, 7)
+    cold_part(0, 7, 8)
+    ccopy1 = table(1)
+    ccopy1.start()
     gather5(1)
     gather3(0)
-    cold_part(0, 7, 8)
     out1 = dhot_out(1)
     out1.start()
     msend.wait()
     m1 = (macc[own, :] + mrecv[:]).astype(BF16)
     xo_ref[:] = (xf + m1.astype(F32) + q1.astype(F32)).astype(BF16)
     gather4(0)
+    ccopy0 = table(0)
+    ccopy0.start()
     gather5(0)
-    wait_bytes(crecv.at[0, pl.ds(0, n_dev - 1)], cr.at[0])
-    ccopy0 = pltpu.make_async_copy(crecv.at[0], cold_ref.at[0], lsem.at[4])
-    ccopy0.start()
     out0 = dhot_out(0)
     out0.start()
-    wait_bytes(idr.at[pl.ds(0, n_dev - 1)], ids_s)
-    wait_bytes(iall.at[pl.ds(0, 3)], hs)
-    wait_bytes(csend.at[pl.ds(0, n_dev - 1)], cs.at[0])
+    wait_bytes(idr.at[head(n_dev - 1)], ids_s)
+    wait_bytes(iall.at[head(3)], hs)
+    wait_bytes(csend.at[head(n_dev - 1)], cs.at[0])
     for l in range(2):
-        wait_bytes(fsend.at[l, pl.ds(0, n_dev - 1)], fs.at[l])
-        wait_bytes(rall.at[l, pl.ds(0, 3)], ash.at[l])
-        wait_bytes(tsend.at[l, pl.ds(0, 15)], ts.at[l])
+        wait_bytes(fsend.at[l, head(n_dev - 1)], fs.at[l])
+        wait_bytes(rall.at[l, head(2)], ash.at[l])
+        wait_bytes(rall.at[l, 0], arl.at[l])
+        wait_bytes(tsend.at[l, head(15)], ts.at[l])
         for ph, n_blk in enumerate((3, 12, 32, 16)):
-            wait_bytes(dh.at[l, pl.ds(0, n_blk), 0], gs.at[l, ph])
+            wait_bytes(dh.at[l, head(n_blk), 0], gs.at[l, ph])
         wait_bytes(dh.at[l, :, 0], ks.at[l])
     for c in (ccopy1, ccopy0, out1, out0):
         c.wait()
 
 
-def finish_body(rid_ref, cold_ref, x_hbm, dhot_hbm, dt_ref, xo_hbm, dho_hbm, xb, hb, sem):
+def finish_body(raw_ref, x_hbm, dhot_hbm, dt_ref, xo_hbm, dho_hbm, xb, hb, sem):
     rows = dt_ref.shape[0] // 4
-    ins = [pltpu.make_async_copy(dhot_hbm.at[l], hb.at[l], sem.at[l]) for l in range(2)]
-    ins.append(pltpu.make_async_copy(x_hbm, xb, sem.at[2]))
+    step, wide = raw_ref.shape[0], raw_ref.shape[1] // 2
+    moves = [(dhot_hbm.at[l], hb.at[l], dho_hbm.at[l]) for l in range(2)] + [(x_hbm, xb, xo_hbm)]
+    ins = [pltpu.make_async_copy(src, buf, sem.at[0, i]) for i, (src, buf, _) in enumerate(moves)]
+    outs = [pltpu.make_async_copy(buf, dst, sem.at[1, i]) for i, (_, buf, dst) in enumerate(moves)]
     for c in ins:
         c.start()
-    ids = jnp.concatenate([rid_ref[g] for g in range(rid_ref.shape[0])], axis=1)
-    outs = [pltpu.make_async_copy(hb.at[l], dho_hbm.at[l], sem.at[3 + l]) for l in range(2)]
-    outs.append(pltpu.make_async_copy(xb, xo_hbm, sem.at[5]))
-    step = 336
     for l in range(2):
-        pc = pieces(cold_ref[l])
-        for r0 in range(0, rows, step):
-            it = lax.broadcasted_iota(I32, (step, ids.shape[1]), 0) + r0
-            oh = jnp.where(it == ids, 1.0, 0.0).astype(BF16)
-            r = dot_nn(oh, pc[0]) + dot_nn(oh, pc[1]) + dot_nn(oh, pc[2])
-            n = min(step, rows - r0)
+        for j in range(4):
+            n = min(step, rows - j * step)
             for t in range(2):
-                dt_ref[pl.ds(r0 * 4 + t * 2 + l, n, stride=4), :] = r[:n, t * 128:(t + 1) * 128]
+                c0 = l * wide + j * 256 + t * 128
+                dt_ref[pl.ds(j * step * 4 + t * 2 + l, n, stride=4), :] = raw_ref[0:n, c0:c0 + 128]
         if l == 0:
             for i, o in zip(ins, outs):
                 i.wait()
@@ -489,7 +515,6 @@
         half = w_up.shape[2] // 2
         fu = half // N_UP
         n_hot = hot_ids.shape[0]
-        n_slots = n_dev * CAP
         me = lax.axis_index('emb')
         hot_match = token_ids[:, None] == hot_ids[None, :]
         hidx = jnp.max(jnp.where(hot_match, jnp.arange(n_hot, dtype=I32)[None, :], -1), axis=1)
@@ -510,22 +535,22 @@
         emb_pad = jnp.pad(emb_table, ((0, 0), (0, -rows_dev % 16), (0, 0)))
 
         VMEM = pltpu.VMEM
-        x_raw, rid, cold, dhot = pl.pallas_call(
+        x_raw, dt_raw, dhot = pl.pallas_call(
             functools.partial(main_body, rows_dev),
-            out_shape=(sds((tok, dim), BF16), sds((n_dev // 16, 1, 128), I32), sds((2, n_dev, CAP, emb), F32),
+            out_shape=(sds((tok, dim), BF16), sds((2 * tok, 8 * emb), F32),
                        sds((2, n_dev // 2, 2, 16, emb), F32)),
-            in_specs=[VM] * 8 + [ANY] * 3, out_specs=(VM, VM, ANY, ANY),
+            in_specs=[VM] * 8 + [ANY] * 3, out_specs=(VM, ANY, ANY),
             scratch_shapes=[VMEM((2 * tok, dim), BF16), VMEM((2 * tok, dim), BF16), VMEM((tok, dim), BF16), VMEM((tok, dim), BF16), VMEM((N_UP, 2 * tok, fu), BF16),
                             VMEM((2 * tok, dim), F32), VMEM((2 * tok, dim), F32), VMEM((tok, dim), F32), VMEM((tok, dim), F32),
                             VMEM((SLOTS, dim, fu), BF16), VMEM((SLOTS, fu, dim), BF16),
                             VMEM((2, tok, emb), F32), VMEM((tok, emb), F32), VMEM((tok, emb), F32),
-                            VMEM((n_dev, 1, 128), I32), VMEM((2, n_dev, 16, 128), BF16), VMEM((2, n_dev, 16, 128), BF16),
+                            VMEM((n_dev // 16, 1, 128), I32), VMEM((n_dev, 1, 128), I32), VMEM((2, n_dev, 16, 128), BF16), VMEM((2, n_dev, 16, 128), BF16),
                             VMEM((n_dev, CAP, emb), F32), VMEM((2, n_dev, CAP, emb), F32),
                             VMEM((2, 4, tok, emb), F32), VMEM((4, 8, tok), I32),
                             VMEM((2, 256, emb), F32), VMEM((2, 256, emb), F32),
                             VMEM((2, 16, 16, emb), F32), VMEM((2, 16, 16, emb), F32),
                             VMEM((2, n_dev // 2, 2, 16, emb), F32),
-                            DMA((2, SLOTS)), DMA((6,)), DMA((6,)), DMA, DMA, DMA, DMA] + [DMA((2,))] * 10
+                            DMA((2, SLOTS)), DMA((6,)), DMA((6,)), DMA, DMA, DMA, DMA] + [DMA((2,))] * 4 + [DMA((2, 3))] + [DMA((2,))] * 6
             + [DMA((2, 4)), DMA((2, 5)), DMA((2,)), DMA((2,)), DMA((5,))],
             compiler_params=pltpu.CompilerParams(collective_id=0, has_side_effects=True, vmem_limit_bytes=VMEM_LIMIT),
             name='stack',
@@ -535,10 +560,10 @@
         d_table, x_out, d_hot = pl.pallas_call(
             finish_body,
             out_shape=(sds((rows_dev * 4, 128), F32), sds((tok, dim), BF16), sds((2, n_hot, emb), F32)),
-            in_specs=[VM, VM, ANY, ANY], out_specs=(VM, ANY, ANY),
-            scratch_shapes=[VMEM((tok, dim), BF16), VMEM((2, n_hot, emb), F32), DMA((6,))],
+            in_specs=[VM, ANY, ANY], out_specs=(VM, ANY, ANY),
+            scratch_shapes=[VMEM((tok, dim), BF16), VMEM((2, n_hot, emb), F32), DMA((2, 3))],
             compiler_params=pltpu.CompilerParams(vmem_limit_bytes=VMEM_LIMIT), name='finish',
-        )(rid, cold.reshape(2, n_slots, emb), x_raw, dhot.reshape(2, n_hot, emb))
+        )(dt_raw, x_raw, dhot.reshape(2, n_hot, emb))
         d_table = d_table.reshape(rows_dev, 2, 2, 128).transpose(2, 0, 1, 3).reshape(2, rows_dev, emb)
         return x_out, d_table, d_hot
 

time: 138 us -> 138 us (level)
  no operation moved by 1% of the time
where the time goes in v3:
time: 138 us; the launch traced here: 137 us
  Pallas kernels  129 us (93%)
  other arithmetic  3.03 us (2%)
  local copies, waits for them, and re-layouts  2.39 us (2%)
    pallas_call x1, Pallas kernels, body(): pl.pallas_call(functools.partial(main_body, rows_dev), out_shape=(sds((to...  123 us
    pallas_call x1, Pallas kernels, body(): pl.pallas_call(finish_body, out_shape=(sds((rows_dev * 4, 128), F32), sds...  6.79 us

profile of v3, /device:TPU:1, one launch (start us, length us, event | category | flops | bytes accessed | tf_op | source)
XLA Modules:
  0.0 137.0 jit_solution(6440470232182230379)
XLA Ops:
  0.6 1.0 select_reduce_fusion
  1.6 0.0 copy-start
  1.6 0.7 and_select_fusion
  2.3 0.7 and_select_fusion.1
  3.0 0.2 convert_reduce_fusion
  3.2 0.5 select_bitcast_fusion
  3.7 0.0 copy-done
  3.7 0.2 fusion.3
  3.9 0.2 fusion.2
  4.2 0.9 fusion
  5.0 1.4 copy.15
  6.4 1.0 pad.4.emb_ref
  7.4 122.6 %stack.1 = (bf16[128,3072]{1,0:T(8,128)(2,1)}, f32[256,2048]{1,0:T(8,128)}, f32[2,64,2,16,256]{4,3,2,1,0:T(8,128)}) custom-call(bf16[128,3072]{1,0:T(8,128)(2,1)} %x_ref.1, s32[128,1,128]{2,1,0:T(1,128)} %bitcast.11, s32[1,128]{1,0:T(1,128)} %get-tuple-element.20.slot_ref, s32[1,128]{1,0:T(1,128)} %bitcast.12, bf16[2,1008,256]{2,1,0:T(8,128)(2,1)} %pad.4.emb_ref, ...), custom_call_target="tpu_custom_call" | custom-call | tf_op jit(solution)/shard_map/stack/pallas_call | solution.py:538
  130.0 6.8 %finish.1 = (f32[4008,128]{1,0:T(8,128)}, bf16[128,3072]{1,0:T(8,128)(2,1)}, f32[2,2048,256]{2,1,0:T(8,128)}) custom-call(f32[256,2048]{1,0:T(8,128)} %get-tuple-element.9.raw_ref, bf16[128,3072]{1,0:T(8,128)(2,1)} %get-tuple-element.10.x_hbm, f32[2,2048,256]{2,1,0:T(8,128)} %bitcast.10), custom_call_target="tpu_custom_call" | custom-call | tf_op jit(solution)/shard_map/finish/pallas_call | solution.py:560
  (1 shorter events, 0.0 us)
Async XLA Ops:
  1.6 2.1 %copy-start = (s32[128]{0:T(128)}, s32[128]{0:T(128)S(1)}, u32[]{:S(2)}) copy-start(s32[128]{0:T(128)S(1)} %select_reduce_fusion) | copy-start | bytes 1540
